TPU v7x, 64 devices: a 2x2x8 block of a 4x4x8 slice. The times are simulated.
64 devices in a mesh: dp: 4 (over x, y), sp: 16 (over z, core).
Axes of the slice: x: 2, y: 2, z: 8, core: 2. Of those that a mesh axis runs over, the one named last changes fastest.
The devices are a block of a 4x4x8 slice.
Arguments:
- signal: bfloat16 [16, 1024, 512], P('dp', 'sp'), parts along dimension 0
- cond_feats: bfloat16 [16, 1024, 128], P('dp', 'sp'), parts along dimension 0
- w_now: bfloat16 [10, 512, 1024], replicated
- w_past: bfloat16 [10, 512, 1024], replicated
- w_cond: bfloat16 [10, 128, 1024], replicated
- b_gate: float32 [10, 1024], replicated
- w_res: bfloat16 [10, 512, 512], replicated
- w_skip: bfloat16 [10, 512, 256], replicated
Outputs:
- output 1: float32 [16, 1024, 512], P('dp', 'sp'), parts along dimension 0
- output 2: float32 [16, 1024, 256], P('dp', 'sp'), parts along dimension 0
There are 4 independent parts. A program takes and returns all parts, laid end to end along the dimension named above; an argument that names none is the same for every part.
All inputs are finite; a program needn't handle non-finite values.
Results may differ from a plain program's by a relative error of at most 0.00672435.
Values are sent between devices in bfloat16 or wider.
A program may use at most 768 MiB of HBM per device.

v0:
```python
import jax
import jax.numpy as jnp
from jax import lax
from jax.sharding import PartitionSpec as P


def solution(mesh):
    seq_devs = mesh.shape['sp']

    def local_stack(signal, cond_feats, w_now, w_past, w_cond, b_gate, w_res, w_skip):
        batch, span_len, channels = signal.shape
        resid = signal.astype(jnp.float32)
        skip_sum = jnp.zeros((batch, span_len, w_skip.shape[2]), jnp.float32)
        for layer in range(w_now.shape[0]):
            dilation = 2 ** layer
            now_in = resid.astype(jnp.bfloat16)
            if dilation < span_len:
                edge_rows = lax.ppermute(now_in[:, span_len - dilation:], 'sp', [(src, src + 1) for src in range(seq_devs - 1)])
                past_in = jnp.concatenate([edge_rows, now_in[:, :span_len - dilation]], axis=1)
            else:
                hop_count = dilation // span_len
                past_in = lax.ppermute(now_in, 'sp', [(src, src + hop_count) for src in range(seq_devs - hop_count)])
            gate_pre = (jnp.einsum('bsc,cg->bsg', now_in, w_now[layer], preferred_element_type=jnp.float32)
                        + jnp.einsum('bsc,cg->bsg', past_in, w_past[layer], preferred_element_type=jnp.float32)
                        + jnp.einsum('bsc,cg->bsg', cond_feats, w_cond[layer], preferred_element_type=jnp.float32)
                        + b_gate[layer])
            gated = (jnp.tanh(gate_pre[..., :channels]) * jax.nn.sigmoid(gate_pre[..., channels:])).astype(jnp.bfloat16)
            resid = resid + jnp.einsum('bsc,cd->bsd', gated, w_res[layer], preferred_element_type=jnp.float32)
            skip_sum = skip_sum + jnp.einsum('bsc,cd->bsd', gated, w_skip[layer], preferred_element_type=jnp.float32)
        return resid, skip_sum

    seq_spec = P('dp', 'sp', None)
    return jax.shard_map(local_stack, mesh=mesh,
                         in_specs=(seq_spec, seq_spec, P(), P(), P(), P(), P(), P()),
                         out_specs=(seq_spec, seq_spec), check_vma=False)
```

profile of v0, /device:TPU:220, one launch (start us, length us, event | category | flops | bytes accessed | tf_op | source)
XLA Modules:
  0.0 111.8 jit_solution(15306970789457758388)
XLA Ops:
  1.5 2.3 %collective-permute-start = (bf16[4,1,512]{2,1,0:T(2,128)(2,1)S(1)}, bf16[4,1,512]{2,1,0:T(2,128)(2,1)S(1)}, u32[]{:S(2)}, u32[]{:S(2)}) collective-permute-start(bf16[4,1,512]{2,1,0:T(2,128)(2,1)S(1)} %slice.277), channel_id=1, source_target_pairs={{0,1},{1,2},{2,3},{3,4},{4,5},{5,6},{6,7},{7,8},{8,9},{9,10},{10,1... | collective-permute-start | bytes 12296 | tf_op jit(solution)/shard_map/ppermute | solution.py:18
  3.9 2.4 %fusion.38 = f32[4,64,1024]{2,1,0:T(8,128)S(1)} fusion(bf16[4,64,512]{2,1,0:T(8,128)(2,1)} %param.8, bf16[10,512,1024]{2,1,0:T(8,128)(2,1)} %param.10), kind=kOutput, calls=%fused_computation.77 | convolution fusion | flops 268435456 | bytes 2359296 | tf_op jit(solution)/shard_map/bsc,cg->bsg/dot_general | solution.py:23
  7.3 1.8 %convolution_add_fusion.19 = f32[4,64,1024]{2,1,0:T(8,128)S(1)} fusion(f32[4,64,1024]{2,1,0:T(8,128)S(1)} %fusion.38, bf16[10,512,1024]{2,1,0:T(8,128)(2,1)} %param.11, bf16[4,63,512]{2,1,0:T(8,128)(2,1)} %bitcast.276, bf16[4,1,512]{2,1,0:T(2,128)(2,1)S(1)} %collective-permute-done), kind=kOutput, calls=%fused_computation.29 | convolution fusion | flops 269221888 | bytes 3411968 | tf_op jit(solution)/shard_map/bsc,cg->bsg/dot_general | solution.py:24
  10.6 1.3 %fusion.197 = (bf16[4,64,512]{2,1,0:T(8,128)(2,1)S(1)}, f32[4,64,512]{2,1,0:T(8,128)S(1)}) fusion(bf16[4,64,512]{2,1,0:T(8,128)(2,1)S(1)} %fusion.120, bf16[10,512,512]{2,1,0:T(8,128)(2,1)} %param.14, bf16[4,64,512]{2,1,0:T(8,128)(2,1)S(1)} %copy-done.6), kind=kOutput, calls=%fused_computation.256 | convolution fusion | flops 134610944 | bytes 1835008 | tf_op jit(solution)/shard_map/bsc,cd->bsd/dot_general | solution.py:28
  12.4 2.8 %collective-permute-start.1 = (bf16[4,2,512]{2,1,0:T(2,128)(2,1)S(1)}, bf16[4,2,512]{2,1,0:T(2,128)(2,1)S(1)}, u32[]{:S(2)}, u32[]{:S(2)}) collective-permute-start(bf16[4,2,512]{2,1,0:T(2,128)(2,1)S(1)} %slice.370), channel_id=1, source_target_pairs={{0,1},{1,2},{2,3},{3,4},{4,5},{5,6},{6,7},{7,8},{8,9},{9,10},{10,1... | collective-permute-start | bytes 24584 | tf_op jit(solution)/shard_map/ppermute | solution.py:18
  16.4 1.3 %collective-permute-done.1 = bf16[4,2,512]{2,1,0:T(2,128)(2,1)S(1)} collective-permute-done((bf16[4,2,512]{2,1,0:T(2,128)(2,1)S(1)}, bf16[4,2,512]{2,1,0:T(2,128)(2,1)S(1)}, u32[]{:S(2)}, u32[]{:S(2)}) %collective-permute-start.1) | collective-permute-done | bytes 8224 | tf_op jit(solution)/shard_map/ppermute | solution.py:18
  17.7 1.8 %convolution_add_fusion.17 = f32[4,64,1024]{2,1,0:T(8,128)S(1)} fusion(f32[4,64,1024]{2,1,0:T(8,128)S(1)} %fusion.35, bf16[10,512,1024]{2,1,0:T(8,128)(2,1)} %param.11, bf16[4,62,512]{2,1,0:T(8,128)(2,1)S(1)} %bitcast.277, bf16[4,2,512]{2,1,0:T(2,128)(2,1)S(1)} %collective-permute-done.1), kind=kOutput, calls=%fused_computation.26 | convolution fusion | flops 269221888 | bytes 3407872 | tf_op jit(solution)/shard_map/bsc,cg->bsg/dot_general | solution.py:24
  19.5 1.6 %fusion.8 = f32[4,64,1024]{2,1,0:T(8,128)S(1)} fusion(f32[4,64,1024]{2,1,0:T(8,128)S(1)} %convolution_add_fusion.17, bf16[4,64,128]{2,1,0:T(8,128)(2,1)S(1)} %copy-done, f32[1024]{0:T(1024)S(1)} %bitcast.286, bf16[10,128,1024]{2,1,0:T(8,128)(2,1)} %param.12), kind=kOutput, calls=%fused_computation.25 | convolution fusion | flops 67633152 | bytes 2428928 | tf_op jit(solution)/shard_map/bsc,cg->bsg/dot_general | solution.py:25
  22.2 2.0 %collective-permute-start.2 = (bf16[4,4,512]{2,1,0:T(4,128)(2,1)S(1)}, bf16[4,4,512]{2,1,0:T(4,128)(2,1)S(1)}, u32[]{:S(2)}, u32[]{:S(2)}) collective-permute-start(bf16[4,4,512]{2,1,0:T(4,128)(2,1)S(1)} %slice.374), channel_id=1, source_target_pairs={{0,1},{1,2},{2,3},{3,4},{4,5},{5,6},{6,7},{7,8},{8,9},{9,10},{10,1... | collective-permute-start | bytes 49160 | tf_op jit(solution)/shard_map/ppermute | solution.py:18
  25.3 1.9 %collective-permute-done.2 = bf16[4,4,512]{2,1,0:T(4,128)(2,1)S(1)} collective-permute-done((bf16[4,4,512]{2,1,0:T(4,128)(2,1)S(1)}, bf16[4,4,512]{2,1,0:T(4,128)(2,1)S(1)}, u32[]{:S(2)}, u32[]{:S(2)}) %collective-permute-start.2) | collective-permute-done | bytes 16416 | tf_op jit(solution)/shard_map/ppermute | solution.py:18
  29.0 2.0 %collective-permute-start.3 = (bf16[4,8,512]{2,1,0:T(8,128)(2,1)S(1)}, bf16[4,8,512]{2,1,0:T(8,128)(2,1)S(1)}, u32[]{:S(2)}, u32[]{:S(2)}) collective-permute-start(bf16[4,8,512]{2,1,0:T(8,128)(2,1)S(1)} %slice.378), channel_id=1, source_target_pairs={{0,1},{1,2},{2,3},{3,4},{4,5},{5,6},{6,7},{7,8},{8,9},{9,10},{10,1... | collective-permute-start | bytes 98312 | tf_op jit(solution)/shard_map/ppermute | solution.py:18
  31.2 3.0 %collective-permute-done.3 = bf16[4,8,512]{2,1,0:T(8,128)(2,1)S(1)} collective-permute-done((bf16[4,8,512]{2,1,0:T(8,128)(2,1)S(1)}, bf16[4,8,512]{2,1,0:T(8,128)(2,1)S(1)}, u32[]{:S(2)}, u32[]{:S(2)}) %collective-permute-start.3) | collective-permute-done | bytes 32800 | tf_op jit(solution)/shard_map/ppermute | solution.py:18
  36.0 2.0 %collective-permute-start.4 = (bf16[4,16,512]{2,1,0:T(8,128)(2,1)S(1)}, bf16[4,16,512]{2,1,0:T(8,128)(2,1)S(1)}, u32[]{:S(2)}, u32[]{:S(2)}) collective-permute-start(bf16[4,16,512]{2,1,0:T(8,128)(2,1)S(1)} %slice.382), channel_id=1, source_target_pairs={{0,1},{1,2},{2,3},{3,4},{4,5},{5,6},{6,7},{7,8},{8,9},{9,10},{10,1... | collective-permute-start | bytes 196616 | tf_op jit(solution)/shard_map/ppermute | solution.py:18
  38.2 3.4 %collective-permute-done.4 = bf16[4,16,512]{2,1,0:T(8,128)(2,1)S(1)} collective-permute-done((bf16[4,16,512]{2,1,0:T(8,128)(2,1)S(1)}, bf16[4,16,512]{2,1,0:T(8,128)(2,1)S(1)}, u32[]{:S(2)}, u32[]{:S(2)}) %collective-permute-start.4) | collective-permute-done | bytes 65568 | tf_op jit(solution)/shard_map/ppermute | solution.py:18
  43.4 2.0 %collective-permute-start.5 = (bf16[4,32,512]{2,1,0:T(8,128)(2,1)S(1)}, bf16[4,32,512]{2,1,0:T(8,128)(2,1)S(1)}, u32[]{:S(2)}, u32[]{:S(2)}) collective-permute-start(bf16[4,32,512]{2,1,0:T(8,128)(2,1)S(1)} %get-tuple-element.2), channel_id=1, source_target_pairs={{0,1},{1,2},{2,3},{3,4},{4,5},{5,6},{6,7},{7,8},{8,9},{9,10},{10,1... | collective-permute-start | bytes 393224 | tf_op jit(solution)/shard_map/ppermute | solution.py:18
  45.5 4.1 %collective-permute-done.5 = bf16[4,32,512]{2,1,0:T(8,128)(2,1)S(1)} collective-permute-done((bf16[4,32,512]{2,1,0:T(8,128)(2,1)S(1)}, bf16[4,32,512]{2,1,0:T(8,128)(2,1)S(1)}, u32[]{:S(2)}, u32[]{:S(2)}) %collective-permute-start.5) | collective-permute-done | bytes 131104 | tf_op jit(solution)/shard_map/ppermute | solution.py:18
  50.9 2.0 %collective-permute-start.6 = (bf16[4,64,512]{2,1,0:T(8,128)(2,1)S(1)}, bf16[4,64,512]{2,1,0:T(8,128)(2,1)S(1)}, u32[]{:S(2)}, u32[]{:S(2)}) collective-permute-start(bf16[4,64,512]{2,1,0:T(8,128)(2,1)S(1)} %get-tuple-element.24), channel_id=1, source_target_pairs={{0,1},{1,2},{2,3},{3,4},{4,5},{5,6},{6,7},{7,8},{8,9},{9,10},{10,1... | collective-permute-start | bytes 786440 | tf_op jit(solution)/shard_map/ppermute | solution.py:22
  53.6 5.1 %collective-permute-done.6 = bf16[4,64,512]{2,1,0:T(8,128)(2,1)S(1)} collective-permute-done((bf16[4,64,512]{2,1,0:T(8,128)(2,1)S(1)}, bf16[4,64,512]{2,1,0:T(8,128)(2,1)S(1)}, u32[]{:S(2)}, u32[]{:S(2)}) %collective-permute-start.6) | collective-permute-done | bytes 262176 | tf_op jit(solution)/shard_map/ppermute | solution.py:22
  59.9 3.3 %collective-permute-start.7 = (bf16[4,64,512]{2,1,0:T(8,128)(2,1)S(1)}, bf16[4,64,512]{2,1,0:T(8,128)(2,1)S(1)}, u32[]{:S(2)}, u32[]{:S(2)}) collective-permute-start(bf16[4,64,512]{2,1,0:T(8,128)(2,1)S(1)} %get-tuple-element.26), channel_id=1, source_target_pairs={{0,2},{1,3},{2,4},{3,5},{4,6},{5,7},{6,8},{7,9},{8,10},{9,11},{10,... | collective-permute-start | bytes 786440 | tf_op jit(solution)/shard_map/ppermute | solution.py:22
  64.0 4.9 %collective-permute-done.7 = bf16[4,64,512]{2,1,0:T(8,128)(2,1)S(1)} collective-permute-done((bf16[4,64,512]{2,1,0:T(8,128)(2,1)S(1)}, bf16[4,64,512]{2,1,0:T(8,128)(2,1)S(1)}, u32[]{:S(2)}, u32[]{:S(2)}) %collective-permute-start.7) | collective-permute-done | bytes 262176 | tf_op jit(solution)/shard_map/ppermute | solution.py:22
  70.2 1.3 %collective-permute-start.8 = (bf16[4,64,512]{2,1,0:T(8,128)(2,1)S(1)}, bf16[4,64,512]{2,1,0:T(8,128)(2,1)S(1)}, u32[]{:S(2)}, u32[]{:S(2)}) collective-permute-start(bf16[4,64,512]{2,1,0:T(8,128)(2,1)S(1)} %get-tuple-element.28), channel_id=1, source_target_pairs={{0,4},{1,5},{2,6},{3,7},{4,8},{5,9},{6,10},{7,11},{8,12},{9,13},{1... | collective-permute-start | bytes 786440 | tf_op jit(solution)/shard_map/ppermute | solution.py:22
  72.2 17.1 %collective-permute-done.8 = bf16[4,64,512]{2,1,0:T(8,128)(2,1)S(1)} collective-permute-done((bf16[4,64,512]{2,1,0:T(8,128)(2,1)S(1)}, bf16[4,64,512]{2,1,0:T(8,128)(2,1)S(1)}, u32[]{:S(2)}, u32[]{:S(2)}) %collective-permute-start.8) | collective-permute-done | bytes 262176 | tf_op jit(solution)/shard_map/ppermute | solution.py:22
  90.5 1.3 %collective-permute-start.9 = (bf16[4,64,512]{2,1,0:T(8,128)(2,1)S(1)}, bf16[4,64,512]{2,1,0:T(8,128)(2,1)S(1)}, u32[]{:S(2)}, u32[]{:S(2)}) collective-permute-start(bf16[4,64,512]{2,1,0:T(8,128)(2,1)S(1)} %get-tuple-element.30), channel_id=1, source_target_pairs={{0,8},{1,9},{2,10},{3,11},{4,12},{5,13},{6,14},{7,15},{16,24},{17,... | collective-permute-start | bytes 786440 | tf_op jit(solution)/shard_map/ppermute | solution.py:22
  92.5 16.3 %collective-permute-done.9 = bf16[4,64,512]{2,1,0:T(8,128)(2,1)S(1)} collective-permute-done((bf16[4,64,512]{2,1,0:T(8,128)(2,1)S(1)}, bf16[4,64,512]{2,1,0:T(8,128)(2,1)S(1)}, u32[]{:S(2)}, u32[]{:S(2)}) %collective-permute-start.9) | collective-permute-done | bytes 262176 | tf_op jit(solution)/shard_map/ppermute | solution.py:22
  (79 shorter events, 23.6 us)
Async XLA Ops:
  0.6 8.5 %copy-start = (bf16[4,64,128]{2,1,0:T(8,128)(2,1)S(1)}, bf16[4,64,128]{2,1,0:T(8,128)(2,1)}, u32[]{:S(2)}) copy-start(bf16[4,64,128]{2,1,0:T(8,128)(2,1)} %param.9) | copy-start | bytes 196612
  0.6 9.9 %copy-start.6 = (bf16[4,64,512]{2,1,0:T(8,128)(2,1)S(1)}, bf16[4,64,512]{2,1,0:T(8,128)(2,1)}, u32[]{:S(2)}) copy-start(bf16[4,64,512]{2,1,0:T(8,128)(2,1)} %param.8) | copy-start | bytes 786436
  1.5 10.5 %copy-start.1 = (bf16[10,512,1024]{2,1,0:T(8,128)(2,1)S(1)}, bf16[10,512,1024]{2,1,0:T(8,128)(2,1)}, u32[]{:S(2)}) copy-start(bf16[10,512,1024]{2,1,0:T(8,128)(2,1)} %param.10) | copy-start | bytes 31457284
  1.5 5.8 %collective-permute-start = (bf16[4,1,512]{2,1,0:T(2,128)(2,1)S(1)}, bf16[4,1,512]{2,1,0:T(2,128)(2,1)S(1)}, u32[]{:S(2)}, u32[]{:S(2)}) collective-permute-start(bf16[4,1,512]{2,1,0:T(2,128)(2,1)S(1)} %slice.277), channel_id=1, source_target_pairs={{0,1},{1,2},{2,3},{3,4},{4,5},{5,6},{6,7},{7,8},{8,9},{9,10},{10,1... | collective-permute-start | bytes 12296 | tf_op jit(solution)/shard_map/ppermute | solution.py:18
  11.9 9.5 %copy-start.3 = (bf16[10,512,512]{2,1,0:T(8,128)(2,1)S(1)}, bf16[10,512,512]{2,1,0:T(8,128)(2,1)}, u32[]{:S(2)}) copy-start(bf16[10,512,512]{2,1,0:T(8,128)(2,1)} %param.14) | copy-start | bytes 15728644
  12.4 5.3 %collective-permute-start.1 = (bf16[4,2,512]{2,1,0:T(2,128)(2,1)S(1)}, bf16[4,2,512]{2,1,0:T(2,128)(2,1)S(1)}, u32[]{:S(2)}, u32[]{:S(2)}) collective-permute-start(bf16[4,2,512]{2,1,0:T(2,128)(2,1)S(1)} %slice.370), channel_id=1, source_target_pairs={{0,1},{1,2},{2,3},{3,4},{4,5},{5,6},{6,7},{7,8},{8,9},{9,10},{10,1... | collective-permute-start | bytes 24584 | tf_op jit(solution)/shard_map/ppermute | solution.py:18
  17.7 9.6 %copy-start.2 = (bf16[10,512,1024]{2,1,0:T(8,128)(2,1)S(1)}, bf16[10,512,1024]{2,1,0:T(8,128)(2,1)}, u32[]{:S(2)}) copy-start(bf16[10,512,1024]{2,1,0:T(8,128)(2,1)} %param.11) | copy-start | bytes 31457284
  21.2 6.6 %copy-start.4 = (bf16[10,128,1024]{2,1,0:T(8,128)(2,1)S(1)}, bf16[10,128,1024]{2,1,0:T(8,128)(2,1)}, u32[]{:S(2)}) copy-start(bf16[10,128,1024]{2,1,0:T(8,128)(2,1)} %param.12) | copy-start | bytes 7864324
  22.2 5.1 %collective-permute-start.2 = (bf16[4,4,512]{2,1,0:T(4,128)(2,1)S(1)}, bf16[4,4,512]{2,1,0:T(4,128)(2,1)S(1)}, u32[]{:S(2)}, u32[]{:S(2)}) collective-permute-start(bf16[4,4,512]{2,1,0:T(4,128)(2,1)S(1)} %slice.374), channel_id=1, source_target_pairs={{0,1},{1,2},{2,3},{3,4},{4,5},{5,6},{6,7},{7,8},{8,9},{9,10},{10,1... | collective-permute-start | bytes 49160 | tf_op jit(solution)/shard_map/ppermute | solution.py:18
  27.3 3.7 %copy-start.5 = (bf16[10,512,256]{2,1,0:T(8,128)(2,1)S(1)}, bf16[10,512,256]{2,1,0:T(8,128)(2,1)}, u32[]{:S(2)}) copy-start(bf16[10,512,256]{2,1,0:T(8,128)(2,1)} %param.15) | copy-start | bytes 7864324
  29.0 5.3 %collective-permute-start.3 = (bf16[4,8,512]{2,1,0:T(8,128)(2,1)S(1)}, bf16[4,8,512]{2,1,0:T(8,128)(2,1)S(1)}, u32[]{:S(2)}, u32[]{:S(2)}) collective-permute-start(bf16[4,8,512]{2,1,0:T(8,128)(2,1)S(1)} %slice.378), channel_id=1, source_target_pairs={{0,1},{1,2},{2,3},{3,4},{4,5},{5,6},{6,7},{7,8},{8,9},{9,10},{10,1... | collective-permute-start | bytes 98312 | tf_op jit(solution)/shard_map/ppermute | solution.py:18
  36.0 5.6 %collective-permute-start.4 = (bf16[4,16,512]{2,1,0:T(8,128)(2,1)S(1)}, bf16[4,16,512]{2,1,0:T(8,128)(2,1)S(1)}, u32[]{:S(2)}, u32[]{:S(2)}) collective-permute-start(bf16[4,16,512]{2,1,0:T(8,128)(2,1)S(1)} %slice.382), channel_id=1, source_target_pairs={{0,1},{1,2},{2,3},{3,4},{4,5},{5,6},{6,7},{7,8},{8,9},{9,10},{10,1... | collective-permute-start | bytes 196616 | tf_op jit(solution)/shard_map/ppermute | solution.py:18
  43.4 6.3 %collective-permute-start.5 = (bf16[4,32,512]{2,1,0:T(8,128)(2,1)S(1)}, bf16[4,32,512]{2,1,0:T(8,128)(2,1)S(1)}, u32[]{:S(2)}, u32[]{:S(2)}) collective-permute-start(bf16[4,32,512]{2,1,0:T(8,128)(2,1)S(1)} %get-tuple-element.2), channel_id=1, source_target_pairs={{0,1},{1,2},{2,3},{3,4},{4,5},{5,6},{6,7},{7,8},{8,9},{9,10},{10,1... | collective-permute-start | bytes 393224 | tf_op jit(solution)/shard_map/ppermute | solution.py:18
  50.9 7.7 %collective-permute-start.6 = (bf16[4,64,512]{2,1,0:T(8,128)(2,1)S(1)}, bf16[4,64,512]{2,1,0:T(8,128)(2,1)S(1)}, u32[]{:S(2)}, u32[]{:S(2)}) collective-permute-start(bf16[4,64,512]{2,1,0:T(8,128)(2,1)S(1)} %get-tuple-element.24), channel_id=1, source_target_pairs={{0,1},{1,2},{2,3},{3,4},{4,5},{5,6},{6,7},{7,8},{8,9},{9,10},{10,1... | collective-permute-start | bytes 786440 | tf_op jit(solution)/shard_map/ppermute | solution.py:22
  59.9 9.0 %collective-permute-start.7 = (bf16[4,64,512]{2,1,0:T(8,128)(2,1)S(1)}, bf16[4,64,512]{2,1,0:T(8,128)(2,1)S(1)}, u32[]{:S(2)}, u32[]{:S(2)}) collective-permute-start(bf16[4,64,512]{2,1,0:T(8,128)(2,1)S(1)} %get-tuple-element.26), channel_id=1, source_target_pairs={{0,2},{1,3},{2,4},{3,5},{4,6},{5,7},{6,8},{7,9},{8,10},{9,11},{10,... | collective-permute-start | bytes 786440 | tf_op jit(solution)/shard_map/ppermute | solution.py:22
  70.2 19.1 %collective-permute-start.8 = (bf16[4,64,512]{2,1,0:T(8,128)(2,1)S(1)}, bf16[4,64,512]{2,1,0:T(8,128)(2,1)S(1)}, u32[]{:S(2)}, u32[]{:S(2)}) collective-permute-start(bf16[4,64,512]{2,1,0:T(8,128)(2,1)S(1)} %get-tuple-element.28), channel_id=1, source_target_pairs={{0,4},{1,5},{2,6},{3,7},{4,8},{5,9},{6,10},{7,11},{8,12},{9,13},{1... | collective-permute-start | bytes 786440 | tf_op jit(solution)/shard_map/ppermute | solution.py:22
  90.5 18.3 %collective-permute-start.9 = (bf16[4,64,512]{2,1,0:T(8,128)(2,1)S(1)}, bf16[4,64,512]{2,1,0:T(8,128)(2,1)S(1)}, u32[]{:S(2)}, u32[]{:S(2)}) collective-permute-start(bf16[4,64,512]{2,1,0:T(8,128)(2,1)S(1)} %get-tuple-element.30), channel_id=1, source_target_pairs={{0,8},{1,9},{2,10},{3,11},{4,12},{5,13},{6,14},{7,15},{16,24},{17,... | collective-permute-start | bytes 786440 | tf_op jit(solution)/shard_map/ppermute | solution.py:22
where the time goes:
time: 112 us
  waiting for transfers between devices  57.2 us (51%)
  matrix products  28.3 us (25%)
  starting transfers between devices  20.8 us (19%)
  other arithmetic  2.14 us (2%)
  local copies, waits for them, and re-layouts  2.05 us (2%)
  between operations  1.32 us (1%)
    ppermute x4, waiting for transfers between devices, local_stack(): lax.ppermute(now_in, 'sp', [(src, src + hop_count) for src in range(seq_d...  43.4 us
    ppermute x6, waiting for transfers between devices, local_stack(): lax.ppermute(now_in[:, span_len - dilation:], 'sp', [(src, src + 1) for s...  13.8 us
    ppermute x6, starting transfers between devices, local_stack(): lax.ppermute(now_in[:, span_len - dilation:], 'sp', [(src, src + 1) for s...  12.9 us
    ppermute x4, starting transfers between devices, local_stack(): lax.ppermute(now_in, 'sp', [(src, src + hop_count) for src in range(seq_d...  7.91 us
    dot_general x10, matrix products, local_stack(): jnp.einsum('bsc,cg->bsg', past_in, w_past[layer], preferred_element_type=...  7.08 us
    dot_general x10, matrix products, local_stack(): jnp.einsum('bsc,cg->bsg', now_in, w_now[layer], preferred_element_type=jn...  6.28 us
    dot_general x10, matrix products, local_stack(): jnp.einsum('bsc,cg->bsg', cond_feats, w_cond[layer], preferred_element_ty...  5.17 us
    dot_general x10, matrix products, local_stack(): jnp.einsum('bsc,cd->bsd', gated, w_skip[layer], preferred_element_type=jn...  4.89 us
  transfers between devices with their start and end apart: 10, of which 9 were waited for; matrix products, arithmetic and copies ran while one was open for 8% of the time, Pallas kernels for 0%

commit v1 on v0

v1 whole, which is shorter than its diff:
```python
import functools

import jax
import jax.numpy as jnp
from jax import lax
from jax.experimental import pallas as pl
from jax.experimental.pallas import tpu as pltpu
from jax.sharding import PartitionSpec as P

MESH = pl.DeviceIdType.MESH
NEAR = 3
RES = 2 ** NEAR
HALO = 16
f32, bf16 = jnp.float32, jnp.bfloat16


def _iota(shape, dim):
    return lax.broadcasted_iota(jnp.int32, shape, dim)


def _kernel(n, sig_hbm, cond_hbm, wn_hbm, wp_hbm, wc_hbm, bg_hbm, wr_hbm, ws_hbm,
            hout_hbm, sout_hbm,
            sig_v, cond_v, halo_s, halo_c, w1, w2, bias,
            hsend, skip0, csend, crecv, hs, orecv, obuf,
            w_sem, in_sem, halo_send, halo_recv, c_send, c_recv, h_send, h_recv, o_send, o_recv, out_sem):
    me = lax.axis_index("sp")
    batch, span, ch = sig_v.shape
    cch = cond_v.shape[2]
    layers = w1.shape[0]
    own = batch * span
    per = span // RES
    ncls = batch * RES
    chunks = ncls // n
    rows = n * per
    wide = w2.shape[2]
    hrows = batch * RES

    ins = [pltpu.make_async_copy(sig_hbm, sig_v, in_sem.at[0]),
           pltpu.make_async_copy(cond_hbm, cond_v, in_sem.at[1]),
           pltpu.make_async_copy(bg_hbm, bias, in_sem.at[2])]
    for c in ins:
        c.start()

    def wcopies(k):
        return [pltpu.make_async_copy(wn_hbm.at[k], w1.at[k, pl.ds(0, ch)], w_sem.at[k, 0]),
                pltpu.make_async_copy(wp_hbm.at[k], w1.at[k, pl.ds(ch, ch)], w_sem.at[k, 1]),
                pltpu.make_async_copy(wc_hbm.at[k], w1.at[k, pl.ds(2 * ch, cch)], w_sem.at[k, 2]),
                pltpu.make_async_copy(wr_hbm.at[k], w2.at[k, :, pl.ds(0, ch)], w_sem.at[k, 3]),
                pltpu.make_async_copy(ws_hbm.at[k], w2.at[k, :, pl.ds(ch, wide - ch)], w_sem.at[k, 4])]

    for k in range(layers):
        for c in wcopies(k):
            c.start()

    barrier = pltpu.get_barrier_semaphore()
    for d in range(1, n):
        pl.semaphore_signal(barrier, inc=1, device_id={"sp": lax.rem(me + d, n)}, device_id_type=MESH)

    ins[0].wait()
    ins[1].wait()
    sig = sig_v[...].reshape(own, ch)
    cnd = cond_v[...].reshape(own, cch)

    r, c = _iota((own, own), 0), _iota((own, own), 1)
    sh_span = span.bit_length() - 1
    sh_per = per.bit_length() - 1
    seq, rho, step = r >> sh_span, (r >> sh_per) & (RES - 1), r & (per - 1)
    perm = (c == seq * span + step * RES + rho).astype(bf16)
    csend[...] = jnp.dot(perm, cnd, preferred_element_type=f32).astype(bf16)
    hsend[...] = jnp.dot(perm, sig, preferred_element_type=f32)

    pl.semaphore_wait(barrier, n - 1)

    def halo_copies():
        nxt = lax.rem(me + 1, n)
        return [pltpu.make_async_remote_copy(sig_v.at[:, pl.ds(span - HALO, HALO)], halo_s, halo_send.at[0],
                                             halo_recv.at[0], device_id={"sp": nxt}, device_id_type=MESH),
                pltpu.make_async_remote_copy(cond_v.at[:, pl.ds(span - HALO, HALO)], halo_c, halo_send.at[1],
                                             halo_recv.at[1], device_id={"sp": nxt}, device_id_type=MESH)]

    for cp in halo_copies():
        cp.start()

    order = [n // 2]
    for d in range(n // 2 - 1, 0, -1):
        order += [n - d, d]
    order += [0]
    crow = chunks * per

    def push(src, dst, send_sem, recv_sem, d, to):
        if d == 0:
            pltpu.make_async_copy(src, dst, recv_sem).start()
        else:
            pltpu.make_async_remote_copy(src, dst, send_sem, recv_sem, device_id={"sp": to},
                                         device_id_type=MESH).start()

    for d in order:
        to = lax.rem(me + d, n)
        push(csend.at[pl.ds(pl.multiple_of(to * crow, crow), crow)], crecv.at[me], c_send, c_recv, d, to)

    for cp in halo_copies():
        cp.wait_recv()
    ins[2].wait()

    hr, hc = _iota((hrows, batch * HALO), 0), _iota((hrows, batch * HALO), 1)
    sh_res = NEAR
    pick = (hc == (hr >> sh_res) * HALO + (HALO - RES) + (hr & (RES - 1))).astype(bf16)
    live = me > 0
    halo_h = jnp.dot(pick, halo_s[...].reshape(batch * HALO, ch), preferred_element_type=f32)
    halo_k = jnp.dot(pick, halo_c[...].reshape(batch * HALO, cch), preferred_element_type=f32).astype(bf16)
    call = jnp.concatenate([csend[...], halo_k], axis=0)
    allr = own + hrows
    half = ch // 2

    def gate(x, k):
        parts = []
        for q in range(2):
            zf = jnp.dot(x, w1[k, :, q * half:(q + 1) * half], preferred_element_type=f32)
            zg = jnp.dot(x, w1[k, :, ch + q * half:ch + (q + 1) * half], preferred_element_type=f32)
            zf = zf + bias[k:k + 1, q * half:(q + 1) * half]
            zg = zg + bias[k:k + 1, ch + q * half:ch + (q + 1) * half]
            parts.append((jnp.tanh(zf) * (0.5 * jnp.tanh(0.5 * zg) + 0.5)).astype(bf16))
        return jnp.concatenate(parts, axis=1)

    for k in range(NEAR):
        d = 2 ** k
        u_own = hsend[...].astype(bf16)
        u_halo = jnp.where(live, halo_h, 0.0).astype(bf16)
        u = jnp.concatenate([u_own, u_halo], axis=0)
        r, c = _iota((allr, allr), 0), _iota((allr, allr), 1)
        seq, rho, step = r >> sh_span, (r >> sh_per) & (RES - 1), r & (per - 1)
        src = step * RES + rho - d
        own_col = seq * span + ((src & (RES - 1)) << sh_per) + (src >> NEAR)
        halo_col = own + seq * RES + src + RES
        col = jnp.where(src >= 0, own_col, halo_col)
        hseq, hrho = (r - own) >> sh_res, (r - own) & (RES - 1)
        col = jnp.where(r < own, col, jnp.where(hrho >= d, own + hseq * RES + hrho - d, -1))
        p = jnp.dot((c == col).astype(bf16), u, preferred_element_type=f32).astype(bf16)
        for cp in wcopies(k):
            cp.wait()
        a = gate(jnp.concatenate([u, p, call], axis=1), k)
        dlt = jnp.dot(a, w2[k], preferred_element_type=f32)
        hsend[...] += dlt[:own, :ch]
        if k == 0:
            skip0[...] = dlt[:own, ch:]
        else:
            skip0[...] += dlt[:own, ch:]
        if k < NEAR - 1:
            halo_h = halo_h + dlt[own:, :ch]

    for ck in range(chunks):
        for d in order:
            to = lax.rem(me + d, n)
            push(hsend.at[pl.ds(pl.multiple_of((to * chunks + ck) * per, per), per)],
                 hs.at[ck, pl.ds(pl.multiple_of(me * per, per), per), pl.ds(0, ch)],
                 h_send, h_recv.at[ck], d, to)

    pltpu.make_async_copy(crecv, crecv, c_recv).wait()
    for k in range(NEAR, layers):
        for cp in wcopies(k):
            cp.wait()

    row = _iota((rows, ch), 0)
    for ck in range(chunks):
        pltpu.make_async_copy(hs.at[ck, :, pl.ds(0, ch)], hs.at[ck, :, pl.ds(0, ch)], h_recv.at[ck]).wait()
        cq = crecv[...].astype(f32)[:, ck * per:(ck + 1) * per].reshape(rows, cch).astype(bf16)
        for k in range(NEAR, layers):
            sft = 2 ** (k - NEAR)
            h = hs[ck, :, 0:ch]
            if sft < 8:
                past = jnp.where(row >= sft, pltpu.roll(h, sft, 0), 0.0)
            else:
                past = jnp.concatenate([jnp.zeros((sft, ch), f32), h[:rows - sft]], axis=0)
            a = gate(jnp.concatenate([h.astype(bf16), past.astype(bf16), cq], axis=1), k)
            dlt = jnp.dot(a, w2[k], preferred_element_type=f32)
            if k == NEAR:
                hs[ck, :, 0:ch] = h + dlt[:, :ch]
                hs[ck, :, ch:wide] = dlt[:, ch:]
            else:
                hs[ck] += dlt
        for d in order:
            to = lax.rem(me + d, n)
            push(hs.at[ck, pl.ds(pl.multiple_of(to * per, per), per)], orecv.at[ck, me],
                 o_send, o_recv.at[ck], d, to)

    for ck in range(chunks):
        pltpu.make_async_copy(orecv.at[ck], orecv.at[ck], o_recv.at[ck]).wait()
        for j in range(n):
            cl = j * chunks + ck
            s, rho = cl // RES, cl % RES
            blk = orecv[ck, j]
            blk = jnp.concatenate([blk[:, :ch], blk[:, ch:] + skip0[cl * per:(cl + 1) * per, :]], axis=1)
            for t in range(wide // 128):
                obuf[t, pl.ds(s * span + rho, per, RES), :] = blk[:, t * 128:(t + 1) * 128]

    outs = []
    for t in range(wide // 128):
        dst = hout_hbm.at[:, pl.ds(t * 128, 128)] if t * 128 < ch else sout_hbm.at[:, pl.ds(t * 128 - ch, 128)]
        outs.append(pltpu.make_async_copy(obuf.at[t], dst, out_sem.at[t]))
        outs[-1].start()
    for cp in outs:
        cp.wait()

    for cp in halo_copies():
        cp.wait_send()
    for buf, sem in ((csend.at[pl.ds(0, own - crow)], c_send), (hsend.at[pl.ds(0, own - crow)], h_send),
                     (hs.at[:, pl.ds(0, rows - per)], o_send)):
        pltpu.make_async_copy(buf, buf, sem).wait()


def solution(mesh):
    n = mesh.shape['sp']

    def local_stack(signal, cond_feats, w_now, w_past, w_cond, b_gate, w_res, w_skip):
        batch, span, ch = signal.shape
        cch = cond_feats.shape[2]
        layers = w_now.shape[0]
        sk = w_skip.shape[2]
        wide = ch + sk
        own = batch * span
        per = span // RES
        chunks = batch * RES // n
        rows = n * per
        any_spec = pl.BlockSpec(memory_space=pl.ANY)
        dma = pltpu.SemaphoreType.DMA
        h_out, skip_out = pl.pallas_call(
            functools.partial(_kernel, n),
            name="stack",
            out_shape=(jax.ShapeDtypeStruct((own, ch), f32), jax.ShapeDtypeStruct((own, sk), f32)),
            in_specs=[any_spec] * 8,
            out_specs=(any_spec, any_spec),
            scratch_shapes=[
                pltpu.VMEM((batch, span, ch), bf16), pltpu.VMEM((batch, span, cch), bf16),
                pltpu.VMEM((batch, HALO, ch), bf16), pltpu.VMEM((batch, HALO, cch), bf16),
                pltpu.VMEM((layers, 2 * ch + cch, 2 * ch), bf16), pltpu.VMEM((layers, ch, wide), bf16),
                pltpu.VMEM((layers, 2 * ch), f32),
                pltpu.VMEM((own, ch), f32), pltpu.VMEM((own, sk), f32),
                pltpu.VMEM((own, cch), bf16), pltpu.VMEM((n, chunks * per, cch), bf16),
                pltpu.VMEM((chunks, rows, wide), f32), pltpu.VMEM((chunks, n, per, wide), f32),
                pltpu.VMEM((wide // 128, own, 128), f32),
                dma((layers, 5)), dma((3,)), dma((2,)), dma((2,)), dma, dma, dma, dma((chunks,)), dma, dma((chunks,)), dma((wide // 128,)),
            ],
            compiler_params=pltpu.CompilerParams(collective_id=0, has_side_effects=True,
                                                 vmem_limit_bytes=60 * 1024 * 1024),
        )(signal, cond_feats, w_now, w_past, w_cond, b_gate, w_res, w_skip)
        return h_out.reshape(batch, span, ch), skip_out.reshape(batch, span, sk)

    seq_spec = P('dp', 'sp', None)
    return jax.shard_map(local_stack, mesh=mesh,
                         in_specs=(seq_spec, seq_spec, P(), P(), P(), P(), P(), P()),
                         out_specs=(seq_spec, seq_spec), check_vma=False)
```

time: 112 us -> 61.9 us (0.55)
  the two profiles are of different devices: /device:TPU:220 before, /device:TPU:21 now
where the time goes in v1:
time: 61.9 us; the launch traced here: 61.8 us
  Pallas kernels  57.6 us (93%)
  local copies, waits for them, and re-layouts  3.54 us (6%)
  between operations  0.64 us (1%)
    pallas_call x1, Pallas kernels, local_stack(): pl.pallas_call(functools.partial(_kernel, n), name='stack', out_shape=(ja...  57.6 us
    unnamed x2, local copies, waits for them, and re-layouts  3.54 us

profile of v1, /device:TPU:21, one launch (start us, length us, event | category | flops | bytes accessed | tf_op | source)
XLA Modules:
  0.0 61.8 jit_solution(5711518552329501298)
XLA Ops:
  0.6 57.6 %stack.1 = (f32[256,512]{1,0:T(8,128)}, f32[256,256]{1,0:T(8,128)}) custom-call(bf16[4,64,512]{2,1,0:T(8,128)(2,1)} %sig_hbm.1, bf16[4,64,128]{2,1,0:T(8,128)(2,1)} %cond_hbm.1, bf16[10,512,1024]{2,1,0:T(8,128)(2,1)} %wn_hbm.1, bf16[10,512,1024]{2,1,0:T(8,128)(2,1)} %wp_hbm.1, bf16[10,128,1024]{2,1,0:T(8,128)(2,1)} %wc_hbm.1, f32[10,1024]{1,0:T(8,128)} %bg_hbm.1, ...), custom_call_target="tpu_custom_call" | custom-call | tf_op jit(solution)/shard_map/stack/pallas_call | solution.py:226
  58.2 1.9 %copy.12 = f32[4,64,512]{2,1,0:T(8,128)} copy(f32[4,64,512]{2,1,0:T(8,128)} %bitcast.2) | data formatting | bytes 1048576
  60.1 1.7 %copy.13 = f32[4,64,256]{2,1,0:T(8,128)} copy(f32[4,64,256]{2,1,0:T(8,128)} %bitcast.3) | data formatting | bytes 524288

commit v2 on v1

v2 whole, which is shorter than its diff:
```python
import functools

import jax
import jax.numpy as jnp
from jax import lax
from jax.experimental import pallas as pl
from jax.experimental.pallas import tpu as pltpu
from jax.sharding import PartitionSpec as P

MESH = pl.DeviceIdType.MESH
NEAR = 3
RES = 2 ** NEAR
HALO = 16
f32, bf16 = jnp.float32, jnp.bfloat16
TRAVEL = f32


def _iota(shape, dim):
    return lax.broadcasted_iota(jnp.int32, shape, dim)


def _stack(n, sig_hbm, cond_hbm, wn_hbm, wp_hbm, wc_hbm, bg_hbm, wr_hbm, ws_hbm,
           recv_hbm, h3_hbm, s3_hbm,
           sig_v, cond_v, halo_s, halo_c, w1, w2, bias,
           near, ssend, csend, dsend, h3, srecv, crecv, drecv, far, osend,
           w_sem, in_sem, halo_send, halo_recv, x_send, x_recv, d_send, d_recv, o_send, o_recv, out_sem):
    me = lax.axis_index("sp")
    batch, span, ch = sig_v.shape
    cch = cond_v.shape[2]
    layers = w1.shape[0]
    own = batch * span
    per = span // RES
    ncls = batch * RES
    chunks = ncls // n
    rows = n * per
    wide = w2.shape[2]
    hrows = batch * RES
    sh_span, sh_per = span.bit_length() - 1, per.bit_length() - 1

    ins = [pltpu.make_async_copy(sig_hbm, sig_v, in_sem.at[0]),
           pltpu.make_async_copy(cond_hbm, cond_v, in_sem.at[1]),
           pltpu.make_async_copy(bg_hbm, bias, in_sem.at[2])]
    for c in ins:
        c.start()

    def wcopies(k):
        return [pltpu.make_async_copy(wn_hbm.at[k], w1.at[k, pl.ds(0, ch)], w_sem.at[k, 0]),
                pltpu.make_async_copy(wp_hbm.at[k], w1.at[k, pl.ds(ch, ch)], w_sem.at[k, 1]),
                pltpu.make_async_copy(wc_hbm.at[k], w1.at[k, pl.ds(2 * ch, cch)], w_sem.at[k, 2]),
                pltpu.make_async_copy(wr_hbm.at[k], w2.at[k, :, pl.ds(0, ch)], w_sem.at[k, 3]),
                pltpu.make_async_copy(ws_hbm.at[k], w2.at[k, :, pl.ds(ch, wide - ch)], w_sem.at[k, 4])]

    for k in range(layers):
        for c in wcopies(k):
            c.start()

    barrier = pltpu.get_barrier_semaphore()
    for d in range(1, n):
        pl.semaphore_signal(barrier, inc=1, device_id={"sp": lax.rem(me + d, n)}, device_id_type=MESH)

    ins[0].wait()
    ins[1].wait()
    r, c = _iota((own, own), 0), _iota((own, own), 1)
    seq, rho, step = r >> sh_span, (r >> sh_per) & (RES - 1), r & (per - 1)
    perm = (c == seq * span + step * RES + rho).astype(bf16)
    cnd = jnp.dot(perm, cond_v[...].reshape(own, cch), preferred_element_type=f32)
    sig = jnp.dot(perm, sig_v[...].reshape(own, ch), preferred_element_type=f32)
    csend[...] = cnd.reshape(n, chunks, per, cch).astype(bf16)
    ssend[...] = sig.reshape(n, chunks, per, ch).astype(bf16)
    h3[...] = sig

    pl.semaphore_wait(barrier, n - 1)

    def halo_copies():
        nxt = lax.rem(me + 1, n)
        return [pltpu.make_async_remote_copy(sig_v.at[:, pl.ds(span - HALO, HALO)], halo_s, halo_send.at[0],
                                             halo_recv.at[0], device_id={"sp": nxt}, device_id_type=MESH),
                pltpu.make_async_remote_copy(cond_v.at[:, pl.ds(span - HALO, HALO)], halo_c, halo_send.at[1],
                                             halo_recv.at[1], device_id={"sp": nxt}, device_id_type=MESH)]

    for cp in halo_copies():
        cp.start()

    order = [n // 2]
    for d in range(n // 2 - 1, 0, -1):
        order += [n - d, d]
    order += [0]

    def push(src, dst, send_sem, recv_sem, d, to):
        if d == 0:
            pltpu.make_async_copy(src, dst, recv_sem).start()
        else:
            pltpu.make_async_remote_copy(src, dst, send_sem, recv_sem, device_id={"sp": to},
                                         device_id_type=MESH).start()

    def drain(buf, sem):
        pltpu.make_async_copy(buf, buf, sem).wait()

    for d in order:
        to = lax.rem(me + d, n)
        push(ssend.at[to], srecv.at[me], x_send.at[0], x_recv.at[0], d, to)
        push(csend.at[to], crecv.at[me], x_send.at[1], x_recv.at[1], d, to)

    for cp in halo_copies():
        cp.wait_recv()
    ins[2].wait()

    hr, hc = _iota((hrows, batch * HALO), 0), _iota((hrows, batch * HALO), 1)
    pick = (hc == (hr >> NEAR) * HALO + (HALO - RES) + (hr & (RES - 1))).astype(bf16)
    live = me > 0
    halo_h = jnp.dot(pick, halo_s[...].reshape(batch * HALO, ch), preferred_element_type=f32)
    halo_k = jnp.dot(pick, halo_c[...].reshape(batch * HALO, cch), preferred_element_type=f32)
    call = jnp.concatenate([cnd, halo_k], axis=0).astype(bf16)
    allr = own + hrows
    half = ch // 2

    def gate(x, k):
        parts = []
        for q in range(2):
            zf = jnp.dot(x, w1[k, :, q * half:(q + 1) * half], preferred_element_type=f32)
            zg = jnp.dot(x, w1[k, :, ch + q * half:ch + (q + 1) * half], preferred_element_type=f32)
            zf = zf + bias[k:k + 1, q * half:(q + 1) * half]
            zg = zg + bias[k:k + 1, ch + q * half:ch + (q + 1) * half]
            parts.append((jnp.tanh(zf) * (0.5 * jnp.tanh(0.5 * zg) + 0.5)).astype(bf16))
        return jnp.concatenate(parts, axis=1)

    for k in range(NEAR):
        d = 2 ** k
        u_halo = jnp.where(live, halo_h, 0.0)
        u = jnp.concatenate([h3[...], u_halo], axis=0).astype(bf16)
        r, c = _iota((allr, allr), 0), _iota((allr, allr), 1)
        seq, rho, step = r >> sh_span, (r >> sh_per) & (RES - 1), r & (per - 1)
        src = step * RES + rho - d
        own_col = seq * span + ((src & (RES - 1)) << sh_per) + (src >> NEAR)
        halo_col = own + seq * RES + src + RES
        col = jnp.where(src >= 0, own_col, halo_col)
        hseq, hrho = (r - own) >> NEAR, (r - own) & (RES - 1)
        col = jnp.where(r < own, col, jnp.where(hrho >= d, own + hseq * RES + hrho - d, -1))
        p = jnp.dot((c == col).astype(bf16), u, preferred_element_type=f32).astype(bf16)
        for cp in wcopies(k):
            cp.wait()
        a = gate(jnp.concatenate([u, p, call], axis=1), k)
        dlt = jnp.dot(a, w2[k], preferred_element_type=f32)
        if k == 0:
            near[...] = dlt[:own]
        else:
            near[...] += dlt[:own]
        h3[...] += dlt[:own, :ch]
        if k < NEAR - 1:
            halo_h = halo_h + dlt[own:, :ch]

    dsend[...] = near[:, 0:ch].reshape(n, chunks, per, ch).astype(TRAVEL)
    for ck in range(chunks):
        for d in order:
            to = lax.rem(me + d, n)
            push(dsend.at[to, ck], drecv.at[ck, me], d_send, d_recv.at[ck], d, to)

    outs = [pltpu.make_async_copy(h3, h3_hbm, out_sem.at[0]),
            pltpu.make_async_copy(near.at[:, pl.ds(ch, wide - ch)], s3_hbm, out_sem.at[1])]
    for cp in outs:
        cp.start()

    drain(srecv, x_recv.at[0])
    drain(crecv, x_recv.at[1])
    for k in range(NEAR, layers):
        for cp in wcopies(k):
            cp.wait()

    row = _iota((rows, ch), 0)
    for ck in range(chunks):
        drain(drecv.at[ck], d_recv.at[ck])
        base = (srecv[:, ck].astype(f32) + drecv[ck].astype(f32)).reshape(rows, ch)
        cq = crecv[:, ck].astype(f32).reshape(rows, cch).astype(bf16)
        h = base
        for k in range(NEAR, layers):
            sft = 2 ** (k - NEAR)
            if k > NEAR:
                h = base + far[:, 0:ch]
            if sft < 8:
                past = jnp.where(row >= sft, pltpu.roll(h, sft, 0), 0.0)
            else:
                past = jnp.concatenate([jnp.zeros((sft, ch), f32), h[:rows - sft]], axis=0)
            a = gate(jnp.concatenate([h.astype(bf16), past.astype(bf16), cq], axis=1), k)
            dlt = jnp.dot(a, w2[k], preferred_element_type=f32)
            if k == NEAR:
                far[...] = dlt
            elif k < layers - 1:
                far[...] += dlt
            else:
                osend[ck] = (far[...] + dlt).reshape(n, per, wide).astype(TRAVEL)
        for d in order:
            to = lax.rem(me + d, n)
            push(osend.at[ck, to], recv_hbm.at[ck, me], o_send, o_recv.at[ck], d, to)

    for cp in halo_copies():
        cp.wait_send()
    for cp in outs:
        cp.wait()
    for buf, sem in ((ssend.at[pl.ds(0, n - 1)], x_send.at[0]), (csend.at[pl.ds(0, n - 1)], x_send.at[1]),
                     (dsend.at[pl.ds(0, n - 1)], d_send), (osend.at[:, pl.ds(0, n - 1)], o_send)):
        drain(buf, sem)
    for ck in range(chunks):
        drain(recv_hbm.at[ck], o_recv.at[ck])


def _finish(recv_hbm, h3_hbm, s3_hbm, hout_hbm, sout_hbm, recv, h3, s3, obuf, in_sem, out_sem):
    chunks, n, per, wide = recv.shape
    own, ch = h3.shape
    span = per * RES
    ins = [pltpu.make_async_copy(h3_hbm, h3, in_sem.at[0]), pltpu.make_async_copy(s3_hbm, s3, in_sem.at[1]),
           pltpu.make_async_copy(recv_hbm, recv, in_sem.at[2])]
    for cp in ins:
        cp.start()
    for cp in ins:
        cp.wait()
    outs = []
    for t in range(wide // 128):
        lo = t * 128
        base, off = (h3, lo) if lo < ch else (s3, lo - ch)
        for ck in range(chunks):
            for j in range(n):
                cl = j * chunks + ck
                s, rho = cl // RES, cl % RES
                obuf[t, pl.ds(s * span + rho, per, RES), :] = (
                    recv[ck, j, :, lo:lo + 128].astype(f32) + base[cl * per:(cl + 1) * per, off:off + 128])
        dst = hout_hbm if lo < ch else sout_hbm
        outs.append(pltpu.make_async_copy(obuf.at[t], dst.at[:, pl.ds(off, 128)], out_sem.at[t]))
        outs[-1].start()
    for cp in outs:
        cp.wait()


def solution(mesh):
    n = mesh.shape['sp']

    def local_stack(signal, cond_feats, w_now, w_past, w_cond, b_gate, w_res, w_skip):
        batch, span, ch = signal.shape
        cch = cond_feats.shape[2]
        layers = w_now.shape[0]
        sk = w_skip.shape[2]
        wide = ch + sk
        own = batch * span
        per = span // RES
        chunks = batch * RES // n
        rows = n * per
        any_spec = pl.BlockSpec(memory_space=pl.ANY)
        dma = pltpu.SemaphoreType.DMA
        sds = jax.ShapeDtypeStruct
        recv, h3, s3 = pl.pallas_call(
            functools.partial(_stack, n),
            name="stack",
            out_shape=(sds((chunks, n, per, wide), TRAVEL), sds((own, ch), f32), sds((own, sk), f32)),
            in_specs=[any_spec] * 8,
            out_specs=(any_spec,) * 3,
            scratch_shapes=[
                pltpu.VMEM((batch, span, ch), bf16), pltpu.VMEM((batch, span, cch), bf16),
                pltpu.VMEM((batch, HALO, ch), bf16), pltpu.VMEM((batch, HALO, cch), bf16),
                pltpu.VMEM((layers, 2 * ch + cch, 2 * ch), bf16), pltpu.VMEM((layers, ch, wide), bf16),
                pltpu.VMEM((layers, 2 * ch), f32),
                pltpu.VMEM((own, wide), f32),
                pltpu.VMEM((n, chunks, per, ch), bf16), pltpu.VMEM((n, chunks, per, cch), bf16),
                pltpu.VMEM((n, chunks, per, ch), TRAVEL), pltpu.VMEM((own, ch), f32),
                pltpu.VMEM((n, chunks, per, ch), bf16), pltpu.VMEM((n, chunks, per, cch), bf16),
                pltpu.VMEM((chunks, n, per, ch), TRAVEL),
                pltpu.VMEM((rows, wide), f32), pltpu.VMEM((chunks, n, per, wide), TRAVEL),
                dma((layers, 5)), dma((3,)), dma((2,)), dma((2,)), dma((2,)), dma((2,)),
                dma, dma((chunks,)), dma, dma((chunks,)), dma((2,)),
            ],
            compiler_params=pltpu.CompilerParams(collective_id=0, has_side_effects=True,
                                                 vmem_limit_bytes=56 * 1024 * 1024),
        )(signal, cond_feats, w_now, w_past, w_cond, b_gate, w_res, w_skip)
        h_out, skip_out = pl.pallas_call(
            _finish,
            name="finish",
            out_shape=(sds((own, ch), f32), sds((own, sk), f32)),
            in_specs=[any_spec] * 3,
            out_specs=(any_spec,) * 2,
            scratch_shapes=[
                pltpu.VMEM((chunks, n, per, wide), TRAVEL), pltpu.VMEM((own, ch), f32), pltpu.VMEM((own, sk), f32),
                pltpu.VMEM((wide // 128, own, 128), f32), dma((3,)), dma((wide // 128,)),
            ],
        )(recv, h3, s3)
        return h_out.reshape(batch, span, ch), skip_out.reshape(batch, span, sk)

    seq_spec = P('dp', 'sp', None)
    return jax.shard_map(local_stack, mesh=mesh,
                         in_specs=(seq_spec, seq_spec, P(), P(), P(), P(), P(), P()),
                         out_specs=(seq_spec, seq_spec), check_vma=False)
```

time: 61.9 us -> 62.8 us (1.015)
  Pallas kernels: 57.6 us -> 62 us
  local copies, waits for them, and re-layouts: 3.54 us -> 0 us
    pallas_call x1 -> x2, Pallas kernels: 57.6 us -> 62 us  [the longest x1 59.7 us: local_stack(): pl.pallas_call(functools.partial(_stack, n), name='stack', out_shape=(sds...]
    unnamed x2 -> x0, local copies, waits for them, and re-layouts: 3.54 us -> none
where the time goes in v2:
time: 62.8 us; the launch traced here: 62.7 us
  Pallas kernels  62 us (99%)
  between operations  0.64 us (1%)
    pallas_call x1, Pallas kernels, local_stack(): pl.pallas_call(functools.partial(_stack, n), name='stack', out_shape=(sds...  59.7 us
    pallas_call x1, Pallas kernels, local_stack(): pl.pallas_call(_finish, name='finish', out_shape=(sds((own, ch), f32), sd...  2.35 us

profile of v2, /device:TPU:21, one launch (start us, length us, event | category | flops | bytes accessed | tf_op | source)
XLA Modules:
  0.0 62.7 jit_solution(9001426154859828071)
XLA Ops:
  0.6 59.7 %stack.1 = (f32[2,16,8,768]{3,2,1,0:T(8,128)}, f32[256,512]{1,0:T(8,128)}, f32[256,256]{1,0:T(8,128)}) custom-call(bf16[4,64,512]{2,1,0:T(8,128)(2,1)} %sig_hbm.1, bf16[4,64,128]{2,1,0:T(8,128)(2,1)} %cond_hbm.1, bf16[10,512,1024]{2,1,0:T(8,128)(2,1)} %wn_hbm.1, bf16[10,512,1024]{2,1,0:T(8,128)(2,1)} %wp_hbm.1, bf16[10,128,1024]{2,1,0:T(8,128)(2,1)} %wc_hbm.1, ...), custom_call_target="tpu_custom_call" | custom-call | tf_op jit(solution)/shard_map/stack/pallas_call | solution.py:249
  60.3 2.4 %finish.1 = (f32[256,512]{1,0:T(8,128)}, f32[256,256]{1,0:T(8,128)}) custom-call(f32[2,16,8,768]{3,2,1,0:T(8,128)} %get-tuple-element.7.recv_hbm, f32[256,512]{1,0:T(8,128)} %get-tuple-element.8.h3_hbm, f32[256,256]{1,0:T(8,128)} %get-tuple-element.9.s3_hbm), custom_call_target="tpu_custom_call" | custom-call | tf_op jit(solution)/shard_map/finish/pallas_call | solution.py:272

commit v3 on v2

--- a/solution.py
+++ b/solution.py
@@ -12,7 +12,7 @@
 RES = 2 ** NEAR
 HALO = 16
 f32, bf16 = jnp.float32, jnp.bfloat16
-TRAVEL = f32
+TRAVEL = bf16
 
 
 def _iota(shape, dim):

time: 62.8 us -> 51.5 us (0.82)
  Pallas kernels: 62 us -> 50.7 us
    pallas_call x1, Pallas kernels: 59.7 us -> 48.5 us  [local_stack(): pl.pallas_call(functools.partial(_stack, n), name='stack', out_shape=(sds...]
where the time goes in v3:
time: 51.5 us; the launch traced here: 51.4 us
  Pallas kernels  50.7 us (98%)
  between operations  0.64 us (1%)
    pallas_call x1, Pallas kernels, local_stack(): pl.pallas_call(functools.partial(_stack, n), name='stack', out_shape=(sds...  48.5 us
    pallas_call x1, Pallas kernels, local_stack(): pl.pallas_call(_finish, name='finish', out_shape=(sds((own, ch), f32), sd...  2.21 us

profile of v3, /device:TPU:21, one launch (start us, length us, event | category | flops | bytes accessed | tf_op | source)
XLA Modules:
  0.0 51.4 jit_solution(11561597894955670008)
XLA Ops:
  0.6 48.5 %stack.1 = (bf16[2,16,8,768]{3,2,1,0:T(8,128)(2,1)}, f32[256,512]{1,0:T(8,128)}, f32[256,256]{1,0:T(8,128)}) custom-call(bf16[4,64,512]{2,1,0:T(8,128)(2,1)} %sig_hbm.1, bf16[4,64,128]{2,1,0:T(8,128)(2,1)} %cond_hbm.1, bf16[10,512,1024]{2,1,0:T(8,128)(2,1)} %wn_hbm.1, bf16[10,512,1024]{2,1,0:T(8,128)(2,1)} %wp_hbm.1, bf16[10,128,1024]{2,1,0:T(8,128)(2,1)} %wc_hbm.1, ...), custom_call_target="tpu_custom_call" | custom-call | tf_op jit(solution)/shard_map/stack/pallas_call | solution.py:249
  49.2 2.2 %finish.1 = (f32[256,512]{1,0:T(8,128)}, f32[256,256]{1,0:T(8,128)}) custom-call(bf16[2,16,8,768]{3,2,1,0:T(8,128)(2,1)} %get-tuple-element.7.recv_hbm, f32[256,512]{1,0:T(8,128)} %get-tuple-element.8.h3_hbm, f32[256,256]{1,0:T(8,128)} %get-tuple-element.9.s3_hbm), custom_call_target="tpu_custom_call" | custom-call | tf_op jit(solution)/shard_map/finish/pallas_call | solution.py:272

commit v4 on v3

--- a/solution.py
+++ b/solution.py
@@ -50,9 +50,12 @@
                 pltpu.make_async_copy(wr_hbm.at[k], w2.at[k, :, pl.ds(0, ch)], w_sem.at[k, 3]),
                 pltpu.make_async_copy(ws_hbm.at[k], w2.at[k, :, pl.ds(ch, wide - ch)], w_sem.at[k, 4])]
 
-    for k in range(layers):
-        for c in wcopies(k):
-            c.start()
+    def fetch(*ks):
+        for k in ks:
+            for c in wcopies(k):
+                c.start()
+
+    fetch(*range(NEAR))
 
     barrier = pltpu.get_barrier_semaphore()
     for d in range(1, n):
@@ -139,6 +142,7 @@
         p = jnp.dot((c == col).astype(bf16), u, preferred_element_type=f32).astype(bf16)
         for cp in wcopies(k):
             cp.wait()
+        fetch(*range(NEAR + 2 * k, min(NEAR + 2 * k + 2, layers - 2)))
         a = gate(jnp.concatenate([u, p, call], axis=1), k)
         dlt = jnp.dot(a, w2[k], preferred_element_type=f32)
         if k == 0:
@@ -155,6 +159,7 @@
             to = lax.rem(me + d, n)
             push(dsend.at[to, ck], drecv.at[ck, me], d_send, d_recv.at[ck], d, to)
 
+    fetch(layers - 2, layers - 1)
     outs = [pltpu.make_async_copy(h3, h3_hbm, out_sem.at[0]),
             pltpu.make_async_copy(near.at[:, pl.ds(ch, wide - ch)], s3_hbm, out_sem.at[1])]
     for cp in outs:
@@ -162,10 +167,6 @@
 
     drain(srecv, x_recv.at[0])
     drain(crecv, x_recv.at[1])
-    for k in range(NEAR, layers):
-        for cp in wcopies(k):
-            cp.wait()
-
     row = _iota((rows, ch), 0)
     for ck in range(chunks):
         drain(drecv.at[ck], d_recv.at[ck])
@@ -180,6 +181,9 @@
                 past = jnp.where(row >= sft, pltpu.roll(h, sft, 0), 0.0)
             else:
                 past = jnp.concatenate([jnp.zeros((sft, ch), f32), h[:rows - sft]], axis=0)
+            if ck == 0:
+                for cp in wcopies(k):
+                    cp.wait()
             a = gate(jnp.concatenate([h.astype(bf16), past.astype(bf16), cq], axis=1), k)
             dlt = jnp.dot(a, w2[k], preferred_element_type=f32)
             if k == NEAR:

time: 51.5 us -> 44.9 us (0.87)
  Pallas kernels: 50.7 us -> 44 us
    pallas_call x1, Pallas kernels: 48.5 us -> 41.8 us  [local_stack(): pl.pallas_call(functools.partial(_stack, n), name='stack', out_shape=(sds...]
where the time goes in v4:
time: 44.9 us; the launch traced here: 44.8 us
  Pallas kernels  44 us (98%)
  between operations  0.8 us (2%)
    pallas_call x1, Pallas kernels, local_stack(): pl.pallas_call(functools.partial(_stack, n), name='stack', out_shape=(sds...  41.8 us
    pallas_call x1, Pallas kernels, local_stack(): pl.pallas_call(_finish, name='finish', out_shape=(sds((own, ch), f32), sd...  2.21 us

profile of v4, /device:TPU:21, one launch (start us, length us, event | category | flops | bytes accessed | tf_op | source)
XLA Modules:
  0.0 44.8 jit_solution(5087887976146881505)
XLA Ops:
  0.6 41.8 %stack.1 = (bf16[2,16,8,768]{3,2,1,0:T(8,128)(2,1)}, f32[256,512]{1,0:T(8,128)}, f32[256,256]{1,0:T(8,128)}) custom-call(bf16[4,64,512]{2,1,0:T(8,128)(2,1)} %sig_hbm.1, bf16[4,64,128]{2,1,0:T(8,128)(2,1)} %cond_hbm.1, bf16[10,512,1024]{2,1,0:T(8,128)(2,1)} %wn_hbm.1, bf16[10,512,1024]{2,1,0:T(8,128)(2,1)} %wp_hbm.1, bf16[10,128,1024]{2,1,0:T(8,128)(2,1)} %wc_hbm.1, ...), custom_call_target="tpu_custom_call" | custom-call | tf_op jit(solution)/shard_map/stack/pallas_call | solution.py:253
  42.4 2.2 %finish.1 = (f32[256,512]{1,0:T(8,128)}, f32[256,256]{1,0:T(8,128)}) custom-call(bf16[2,16,8,768]{3,2,1,0:T(8,128)(2,1)} %get-tuple-element.7.recv_hbm, f32[256,512]{1,0:T(8,128)} %get-tuple-element.8.h3_hbm, f32[256,256]{1,0:T(8,128)} %get-tuple-element.9.s3_hbm), custom_call_target="tpu_custom_call" | custom-call | tf_op jit(solution)/shard_map/finish/pallas_call | solution.py:276

commit v5 on v4

--- a/solution.py
+++ b/solution.py
@@ -23,7 +23,7 @@
            recv_hbm, h3_hbm, s3_hbm,
            sig_v, cond_v, halo_s, halo_c, w1, w2, bias,
            near, ssend, csend, dsend, h3, srecv, crecv, drecv, far, osend,
-           w_sem, in_sem, halo_send, halo_recv, x_send, x_recv, d_send, d_recv, o_send, o_recv, out_sem):
+           w_sem, in_sem, halo_send, halo_recv, x_send, x_recv, d_send, d_recv, o_send, o_recv, out_sem, round_sem):
     me = lax.axis_index("sp")
     batch, span, ch = sig_v.shape
     cch = cond_v.shape[2]
@@ -37,6 +37,13 @@
     hrows = batch * RES
     sh_span, sh_per = span.bit_length() - 1, per.bit_length() - 1
 
+    def tell(sem, d):
+        for to in (lax.rem(me + d, n), lax.rem(me + n - d, n)):
+            pl.semaphore_signal(sem, inc=1, device_id={"sp": to}, device_id_type=MESH)
+
+    barrier = pltpu.get_barrier_semaphore()
+    tell(barrier, 1)
+
     ins = [pltpu.make_async_copy(sig_hbm, sig_v, in_sem.at[0]),
            pltpu.make_async_copy(cond_hbm, cond_v, in_sem.at[1]),
            pltpu.make_async_copy(bg_hbm, bias, in_sem.at[2])]
@@ -55,14 +62,22 @@
             for c in wcopies(k):
                 c.start()
 
-    fetch(*range(NEAR))
-
-    barrier = pltpu.get_barrier_semaphore()
-    for d in range(1, n):
-        pl.semaphore_signal(barrier, inc=1, device_id={"sp": lax.rem(me + d, n)}, device_id_type=MESH)
-
+    fetch(0)
+
+    def halo_copies():
+        nxt = lax.rem(me + 1, n)
+        return [pltpu.make_async_remote_copy(sig_v.at[:, pl.ds(span - HALO, HALO)], halo_s, halo_send.at[0],
+                                             halo_recv.at[0], device_id={"sp": nxt}, device_id_type=MESH),
+                pltpu.make_async_remote_copy(cond_v.at[:, pl.ds(span - HALO, HALO)], halo_c, halo_send.at[1],
+                                             halo_recv.at[1], device_id={"sp": nxt}, device_id_type=MESH)]
+
+    pl.semaphore_wait(barrier, 2)
     ins[0].wait()
     ins[1].wait()
+    for cp in halo_copies():
+        cp.start()
+    tell(round_sem.at[0], 1)
+    fetch(1, 2)
     r, c = _iota((own, own), 0), _iota((own, own), 1)
     seq, rho, step = r >> sh_span, (r >> sh_per) & (RES - 1), r & (per - 1)
     perm = (c == seq * span + step * RES + rho).astype(bf16)
@@ -72,17 +87,14 @@
     ssend[...] = sig.reshape(n, chunks, per, ch).astype(bf16)
     h3[...] = sig
 
-    pl.semaphore_wait(barrier, n - 1)
-
-    def halo_copies():
-        nxt = lax.rem(me + 1, n)
-        return [pltpu.make_async_remote_copy(sig_v.at[:, pl.ds(span - HALO, HALO)], halo_s, halo_send.at[0],
-                                             halo_recv.at[0], device_id={"sp": nxt}, device_id_type=MESH),
-                pltpu.make_async_remote_copy(cond_v.at[:, pl.ds(span - HALO, HALO)], halo_c, halo_send.at[1],
-                                             halo_recv.at[1], device_id={"sp": nxt}, device_id_type=MESH)]
-
-    for cp in halo_copies():
-        cp.start()
+    reach, rnd = 2, 0
+    while True:
+        pl.semaphore_wait(round_sem.at[rnd], 2)
+        if reach >= n // 2:
+            break
+        rnd += 1
+        tell(round_sem.at[rnd], reach)
+        reach *= 2
 
     order = [n // 2]
     for d in range(n // 2 - 1, 0, -1):
@@ -101,8 +113,9 @@
 
     for d in order:
         to = lax.rem(me + d, n)
-        push(ssend.at[to], srecv.at[me], x_send.at[0], x_recv.at[0], d, to)
-        push(csend.at[to], crecv.at[me], x_send.at[1], x_recv.at[1], d, to)
+        push(csend.at[to], crecv.at[me], x_send.at[chunks], x_recv.at[chunks], d, to)
+        push(ssend.at[to, 0], srecv.at[0, me], x_send.at[0], x_recv.at[0], d, to)
+    fetch(NEAR, NEAR + 1)
 
     for cp in halo_copies():
         cp.wait_recv()
@@ -142,7 +155,6 @@
         p = jnp.dot((c == col).astype(bf16), u, preferred_element_type=f32).astype(bf16)
         for cp in wcopies(k):
             cp.wait()
-        fetch(*range(NEAR + 2 * k, min(NEAR + 2 * k + 2, layers - 2)))
         a = gate(jnp.concatenate([u, p, call], axis=1), k)
         dlt = jnp.dot(a, w2[k], preferred_element_type=f32)
         if k == 0:
@@ -157,20 +169,24 @@
     for ck in range(chunks):
         for d in order:
             to = lax.rem(me + d, n)
+            if ck > 0:
+                push(ssend.at[to, ck], srecv.at[ck, me], x_send.at[ck], x_recv.at[ck], d, to)
             push(dsend.at[to, ck], drecv.at[ck, me], d_send, d_recv.at[ck], d, to)
-
-    fetch(layers - 2, layers - 1)
+        if ck == 0:
+            fetch(NEAR + 2, NEAR + 3)
+
+    fetch(*range(NEAR + 4, layers))
     outs = [pltpu.make_async_copy(h3, h3_hbm, out_sem.at[0]),
             pltpu.make_async_copy(near.at[:, pl.ds(ch, wide - ch)], s3_hbm, out_sem.at[1])]
     for cp in outs:
         cp.start()
 
-    drain(srecv, x_recv.at[0])
-    drain(crecv, x_recv.at[1])
+    drain(crecv, x_recv.at[chunks])
     row = _iota((rows, ch), 0)
     for ck in range(chunks):
+        drain(srecv.at[ck], x_recv.at[ck])
         drain(drecv.at[ck], d_recv.at[ck])
-        base = (srecv[:, ck].astype(f32) + drecv[ck].astype(f32)).reshape(rows, ch)
+        base = (srecv[ck].astype(f32) + drecv[ck].astype(f32)).reshape(rows, ch)
         cq = crecv[:, ck].astype(f32).reshape(rows, cch).astype(bf16)
         h = base
         for k in range(NEAR, layers):
@@ -200,8 +216,9 @@
         cp.wait_send()
     for cp in outs:
         cp.wait()
-    for buf, sem in ((ssend.at[pl.ds(0, n - 1)], x_send.at[0]), (csend.at[pl.ds(0, n - 1)], x_send.at[1]),
-                     (dsend.at[pl.ds(0, n - 1)], d_send), (osend.at[:, pl.ds(0, n - 1)], o_send)):
+    for ck in range(chunks):
+        drain(ssend.at[pl.ds(0, n - 1), ck], x_send.at[ck])
+    for buf, sem in ((csend.at[pl.ds(0, n - 1)], x_send.at[chunks]), (dsend.at[pl.ds(0, n - 1)], d_send), (osend.at[:, pl.ds(0, n - 1)], o_send)):
         drain(buf, sem)
     for ck in range(chunks):
         drain(recv_hbm.at[ck], o_recv.at[ck])
@@ -264,11 +281,11 @@
                 pltpu.VMEM((own, wide), f32),
                 pltpu.VMEM((n, chunks, per, ch), bf16), pltpu.VMEM((n, chunks, per, cch), bf16),
                 pltpu.VMEM((n, chunks, per, ch), TRAVEL), pltpu.VMEM((own, ch), f32),
-                pltpu.VMEM((n, chunks, per, ch), bf16), pltpu.VMEM((n, chunks, per, cch), bf16),
+                pltpu.VMEM((chunks, n, per, ch), bf16), pltpu.VMEM((n, chunks, per, cch), bf16),
                 pltpu.VMEM((chunks, n, per, ch), TRAVEL),
                 pltpu.VMEM((rows, wide), f32), pltpu.VMEM((chunks, n, per, wide), TRAVEL),
-                dma((layers, 5)), dma((3,)), dma((2,)), dma((2,)), dma((2,)), dma((2,)),
-                dma, dma((chunks,)), dma, dma((chunks,)), dma((2,)),
+                dma((layers, 5)), dma((3,)), dma((2,)), dma((2,)), dma((chunks + 1,)), dma((chunks + 1,)),
+                dma, dma((chunks,)), dma, dma((chunks,)), dma((2,)), pltpu.SemaphoreType.REGULAR((4,)),
             ],
             compiler_params=pltpu.CompilerParams(collective_id=0, has_side_effects=True,
                                                  vmem_limit_bytes=56 * 1024 * 1024),

time: 44.9 us -> 45.3 us (level)
  no operation moved by 1% of the time
where the time goes in v5:
time: 45.3 us; the launch traced here: 45.2 us
  Pallas kernels  44.4 us (98%)
  between operations  0.8 us (2%)
    pallas_call x1, Pallas kernels, local_stack(): pl.pallas_call(functools.partial(_stack, n), name='stack', out_shape=(sds...  42.2 us
    pallas_call x1, Pallas kernels, local_stack(): pl.pallas_call(_finish, name='finish', out_shape=(sds((own, ch), f32), sd...  2.21 us

profile of v5, /device:TPU:21, one launch (start us, length us, event | category | flops | bytes accessed | tf_op | source)
XLA Modules:
  0.0 45.2 jit_solution(2023286024678075673)
XLA Ops:
  0.6 42.2 %stack.1 = (bf16[2,16,8,768]{3,2,1,0:T(8,128)(2,1)}, f32[256,512]{1,0:T(8,128)}, f32[256,256]{1,0:T(8,128)}) custom-call(bf16[4,64,512]{2,1,0:T(8,128)(2,1)} %sig_hbm.1, bf16[4,64,128]{2,1,0:T(8,128)(2,1)} %cond_hbm.1, bf16[10,512,1024]{2,1,0:T(8,128)(2,1)} %wn_hbm.1, bf16[10,512,1024]{2,1,0:T(8,128)(2,1)} %wp_hbm.1, bf16[10,128,1024]{2,1,0:T(8,128)(2,1)} %wc_hbm.1, ...), custom_call_target="tpu_custom_call" | custom-call | tf_op jit(solution)/shard_map/stack/pallas_call | solution.py:270
  42.8 2.2 %finish.1 = (f32[256,512]{1,0:T(8,128)}, f32[256,256]{1,0:T(8,128)}) custom-call(bf16[2,16,8,768]{3,2,1,0:T(8,128)(2,1)} %get-tuple-element.7.recv_hbm, f32[256,512]{1,0:T(8,128)} %get-tuple-element.8.h3_hbm, f32[256,256]{1,0:T(8,128)} %get-tuple-element.9.s3_hbm), custom_call_target="tpu_custom_call" | custom-call | tf_op jit(solution)/shard_map/finish/pallas_call | solution.py:293

commit v6 on v5

--- a/solution.py
+++ b/solution.py
@@ -20,10 +20,10 @@
 
 
 def _stack(n, sig_hbm, cond_hbm, wn_hbm, wp_hbm, wc_hbm, bg_hbm, wr_hbm, ws_hbm,
-           recv_hbm, h3_hbm, s3_hbm,
+           recv, h3, s3,
            sig_v, cond_v, halo_s, halo_c, w1, w2, bias,
-           near, ssend, csend, dsend, h3, srecv, crecv, drecv, far, osend,
-           w_sem, in_sem, halo_send, halo_recv, x_send, x_recv, d_send, d_recv, o_send, o_recv, out_sem, round_sem):
+           near, ssend, csend, dsend, srecv, crecv, drecv, far, osend,
+           w_sem, in_sem, halo_send, halo_recv, x_send, x_recv, d_send, d_recv, o_send, o_recv):
     me = lax.axis_index("sp")
     batch, span, ch = sig_v.shape
     cch = cond_v.shape[2]
@@ -37,12 +37,9 @@
     hrows = batch * RES
     sh_span, sh_per = span.bit_length() - 1, per.bit_length() - 1
 
-    def tell(sem, d):
-        for to in (lax.rem(me + d, n), lax.rem(me + n - d, n)):
-            pl.semaphore_signal(sem, inc=1, device_id={"sp": to}, device_id_type=MESH)
-
     barrier = pltpu.get_barrier_semaphore()
-    tell(barrier, 1)
+    for d in range(1, n):
+        pl.semaphore_signal(barrier, inc=1, device_id={"sp": lax.rem(me + d, n)}, device_id_type=MESH)
 
     ins = [pltpu.make_async_copy(sig_hbm, sig_v, in_sem.at[0]),
            pltpu.make_async_copy(cond_hbm, cond_v, in_sem.at[1]),
@@ -71,13 +68,9 @@
                 pltpu.make_async_remote_copy(cond_v.at[:, pl.ds(span - HALO, HALO)], halo_c, halo_send.at[1],
                                              halo_recv.at[1], device_id={"sp": nxt}, device_id_type=MESH)]
 
-    pl.semaphore_wait(barrier, 2)
+    fetch(1, 2)
     ins[0].wait()
     ins[1].wait()
-    for cp in halo_copies():
-        cp.start()
-    tell(round_sem.at[0], 1)
-    fetch(1, 2)
     r, c = _iota((own, own), 0), _iota((own, own), 1)
     seq, rho, step = r >> sh_span, (r >> sh_per) & (RES - 1), r & (per - 1)
     perm = (c == seq * span + step * RES + rho).astype(bf16)
@@ -87,14 +80,9 @@
     ssend[...] = sig.reshape(n, chunks, per, ch).astype(bf16)
     h3[...] = sig
 
-    reach, rnd = 2, 0
-    while True:
-        pl.semaphore_wait(round_sem.at[rnd], 2)
-        if reach >= n // 2:
-            break
-        rnd += 1
-        tell(round_sem.at[rnd], reach)
-        reach *= 2
+    pl.semaphore_wait(barrier, n - 1)
+    for cp in halo_copies():
+        cp.start()
 
     order = [n // 2]
     for d in range(n // 2 - 1, 0, -1):
@@ -158,14 +146,16 @@
         a = gate(jnp.concatenate([u, p, call], axis=1), k)
         dlt = jnp.dot(a, w2[k], preferred_element_type=f32)
         if k == 0:
-            near[...] = dlt[:own]
+            near[...] = dlt[:own, :ch]
+            s3[...] = dlt[:own, ch:]
         else:
-            near[...] += dlt[:own]
+            near[...] += dlt[:own, :ch]
+            s3[...] += dlt[:own, ch:]
         h3[...] += dlt[:own, :ch]
         if k < NEAR - 1:
             halo_h = halo_h + dlt[own:, :ch]
 
-    dsend[...] = near[:, 0:ch].reshape(n, chunks, per, ch).astype(TRAVEL)
+    dsend[...] = near[...].reshape(n, chunks, per, ch).astype(TRAVEL)
     for ck in range(chunks):
         for d in order:
             to = lax.rem(me + d, n)
@@ -176,11 +166,6 @@
             fetch(NEAR + 2, NEAR + 3)
 
     fetch(*range(NEAR + 4, layers))
-    outs = [pltpu.make_async_copy(h3, h3_hbm, out_sem.at[0]),
-            pltpu.make_async_copy(near.at[:, pl.ds(ch, wide - ch)], s3_hbm, out_sem.at[1])]
-    for cp in outs:
-        cp.start()
-
     drain(crecv, x_recv.at[chunks])
     row = _iota((rows, ch), 0)
     for ck in range(chunks):
@@ -210,30 +195,22 @@
                 osend[ck] = (far[...] + dlt).reshape(n, per, wide).astype(TRAVEL)
         for d in order:
             to = lax.rem(me + d, n)
-            push(osend.at[ck, to], recv_hbm.at[ck, me], o_send, o_recv.at[ck], d, to)
+            push(osend.at[ck, to], recv.at[ck, me], o_send, o_recv.at[ck], d, to)
 
     for cp in halo_copies():
         cp.wait_send()
-    for cp in outs:
-        cp.wait()
     for ck in range(chunks):
         drain(ssend.at[pl.ds(0, n - 1), ck], x_send.at[ck])
     for buf, sem in ((csend.at[pl.ds(0, n - 1)], x_send.at[chunks]), (dsend.at[pl.ds(0, n - 1)], d_send), (osend.at[:, pl.ds(0, n - 1)], o_send)):
         drain(buf, sem)
     for ck in range(chunks):
-        drain(recv_hbm.at[ck], o_recv.at[ck])
-
-
-def _finish(recv_hbm, h3_hbm, s3_hbm, hout_hbm, sout_hbm, recv, h3, s3, obuf, in_sem, out_sem):
+        drain(recv.at[ck], o_recv.at[ck])
+
+
+def _finish(recv, h3, s3, hout_hbm, sout_hbm, obuf, out_sem):
     chunks, n, per, wide = recv.shape
     own, ch = h3.shape
     span = per * RES
-    ins = [pltpu.make_async_copy(h3_hbm, h3, in_sem.at[0]), pltpu.make_async_copy(s3_hbm, s3, in_sem.at[1]),
-           pltpu.make_async_copy(recv_hbm, recv, in_sem.at[2])]
-    for cp in ins:
-        cp.start()
-    for cp in ins:
-        cp.wait()
     outs = []
     for t in range(wide // 128):
         lo = t * 128
@@ -270,22 +247,22 @@
         recv, h3, s3 = pl.pallas_call(
             functools.partial(_stack, n),
             name="stack",
-            out_shape=(sds((chunks, n, per, wide), TRAVEL), sds((own, ch), f32), sds((own, sk), f32)),
+            out_shape=(pltpu.VMEM((chunks, n, per, wide), TRAVEL), pltpu.VMEM((own, ch), f32), pltpu.VMEM((own, sk), f32)),
             in_specs=[any_spec] * 8,
-            out_specs=(any_spec,) * 3,
+            out_specs=(pl.BlockSpec(memory_space=pltpu.VMEM),) * 3,
             scratch_shapes=[
                 pltpu.VMEM((batch, span, ch), bf16), pltpu.VMEM((batch, span, cch), bf16),
                 pltpu.VMEM((batch, HALO, ch), bf16), pltpu.VMEM((batch, HALO, cch), bf16),
                 pltpu.VMEM((layers, 2 * ch + cch, 2 * ch), bf16), pltpu.VMEM((layers, ch, wide), bf16),
                 pltpu.VMEM((layers, 2 * ch), f32),
-                pltpu.VMEM((own, wide), f32),
+                pltpu.VMEM((own, ch), f32),
                 pltpu.VMEM((n, chunks, per, ch), bf16), pltpu.VMEM((n, chunks, per, cch), bf16),
-                pltpu.VMEM((n, chunks, per, ch), TRAVEL), pltpu.VMEM((own, ch), f32),
+                pltpu.VMEM((n, chunks, per, ch), TRAVEL),
                 pltpu.VMEM((chunks, n, per, ch), bf16), pltpu.VMEM((n, chunks, per, cch), bf16),
                 pltpu.VMEM((chunks, n, per, ch), TRAVEL),
                 pltpu.VMEM((rows, wide), f32), pltpu.VMEM((chunks, n, per, wide), TRAVEL),
                 dma((layers, 5)), dma((3,)), dma((2,)), dma((2,)), dma((chunks + 1,)), dma((chunks + 1,)),
-                dma, dma((chunks,)), dma, dma((chunks,)), dma((2,)), pltpu.SemaphoreType.REGULAR((4,)),
+                dma, dma((chunks,)), dma, dma((chunks,)),
             ],
             compiler_params=pltpu.CompilerParams(collective_id=0, has_side_effects=True,
                                                  vmem_limit_bytes=56 * 1024 * 1024),
@@ -294,13 +271,12 @@
             _finish,
             name="finish",
             out_shape=(sds((own, ch), f32), sds((own, sk), f32)),
-            in_specs=[any_spec] * 3,
+            in_specs=[pl.BlockSpec(memory_space=pltpu.VMEM)] * 3,
             out_specs=(any_spec,) * 2,
             scratch_shapes=[
-                pltpu.VMEM((chunks, n, per, wide), TRAVEL), pltpu.VMEM((own, ch), f32), pltpu.VMEM((own, sk), f32),
-                pltpu.VMEM((wide // 128, own, 128), f32), dma((3,)), dma((wide // 128,)),
+                pltpu.VMEM((wide // 128, own, 128), f32), dma((wide // 128,)),
             ],
-        )(recv, h3, s3)
+        )(*(pltpu.with_memory_space_constraint(x, pltpu.VMEM) for x in (recv, h3, s3)))
         return h_out.reshape(batch, span, ch), skip_out.reshape(batch, span, sk)
 
     seq_spec = P('dp', 'sp', None)

time: 45.3 us -> 43.7 us (0.965)
  Pallas kernels: 44.4 us -> 42.9 us
    pallas_call x1, Pallas kernels: 2.21 us -> 0.95 us  [local_stack(): pl.pallas_call(_finish, name='finish', out_shape=(sds((own, ch), f32), sd...]
where the time goes in v6:
time: 43.7 us; the launch traced here: 43.6 us
  Pallas kernels  42.9 us (98%)
  between operations  0.64 us (1%)
    pallas_call x1, Pallas kernels, local_stack(): pl.pallas_call(functools.partial(_stack, n), name='stack', out_shape=(plt...  42 us
    pallas_call x1, Pallas kernels, local_stack(): pl.pallas_call(_finish, name='finish', out_shape=(sds((own, ch), f32), sd...  0.95 us

profile of v6, /device:TPU:21, one launch (start us, length us, event | category | flops | bytes accessed | tf_op | source)
XLA Modules:
  0.0 43.6 jit_solution(5390352749571596847)
XLA Ops:
  0.6 42.0 %stack.1 = (bf16[2,16,8,768]{3,2,1,0:T(8,128)(2,1)S(1)}, f32[256,512]{1,0:T(8,128)S(1)}, f32[256,256]{1,0:T(8,128)S(1)}) custom-call(bf16[4,64,512]{2,1,0:T(8,128)(2,1)} %sig_hbm.1, bf16[4,64,128]{2,1,0:T(8,128)(2,1)} %cond_hbm.1, bf16[10,512,1024]{2,1,0:T(8,128)(2,1)} %wn_hbm.1, bf16[10,512,1024]{2,1,0:T(8,128)(2,1)} %wp_hbm.1, ...), custom_call_target="tpu_custom_call" | custom-call | tf_op jit(solution)/shard_map/stack/pallas_call | solution.py:247
  42.6 1.0 %finish.1 = (f32[256,512]{1,0:T(8,128)}, f32[256,256]{1,0:T(8,128)}) custom-call(bf16[2,16,8,768]{3,2,1,0:T(8,128)(2,1)S(1)} %get-tuple-element.7.recv, f32[256,512]{1,0:T(8,128)S(1)} %get-tuple-element.8.h3, f32[256,256]{1,0:T(8,128)S(1)} %get-tuple-element.9.s3), custom_call_target="tpu_custom_call" | custom-call | tf_op jit(solution)/shard_map/finish/pallas_call | solution.py:270

commit v7 on v6

--- a/solution.py
+++ b/solution.py
@@ -21,7 +21,7 @@
 
 def _stack(n, sig_hbm, cond_hbm, wn_hbm, wp_hbm, wc_hbm, bg_hbm, wr_hbm, ws_hbm,
            recv, h3, s3,
-           sig_v, cond_v, halo_s, halo_c, w1, w2, bias,
+           sig_v, cond_v, halo_s, halo_c, w1, wc, w2, bias, zc, gates,
            near, ssend, csend, dsend, srecv, crecv, drecv, far, osend,
            w_sem, in_sem, halo_send, halo_recv, x_send, x_recv, d_send, d_recv, o_send, o_recv):
     me = lax.axis_index("sp")
@@ -50,15 +50,19 @@
     def wcopies(k):
         return [pltpu.make_async_copy(wn_hbm.at[k], w1.at[k, pl.ds(0, ch)], w_sem.at[k, 0]),
                 pltpu.make_async_copy(wp_hbm.at[k], w1.at[k, pl.ds(ch, ch)], w_sem.at[k, 1]),
-                pltpu.make_async_copy(wc_hbm.at[k], w1.at[k, pl.ds(2 * ch, cch)], w_sem.at[k, 2]),
-                pltpu.make_async_copy(wr_hbm.at[k], w2.at[k, :, pl.ds(0, ch)], w_sem.at[k, 3]),
-                pltpu.make_async_copy(ws_hbm.at[k], w2.at[k, :, pl.ds(ch, wide - ch)], w_sem.at[k, 4])]
+                pltpu.make_async_copy(wr_hbm.at[k], w2.at[k, :, pl.ds(0, ch)], w_sem.at[k, 2]),
+                pltpu.make_async_copy(ws_hbm.at[k], w2.at[k, :, pl.ds(ch, wide - ch)], w_sem.at[k, 3])]
+
+    def ccopy(k):
+        return pltpu.make_async_copy(wc_hbm.at[k], wc.at[k], w_sem.at[k, 4])
 
     def fetch(*ks):
         for k in ks:
             for c in wcopies(k):
                 c.start()
 
+    for k in range(NEAR):
+        ccopy(k).start()
     fetch(0)
 
     def halo_copies():
@@ -68,7 +72,9 @@
                 pltpu.make_async_remote_copy(cond_v.at[:, pl.ds(span - HALO, HALO)], halo_c, halo_send.at[1],
                                              halo_recv.at[1], device_id={"sp": nxt}, device_id_type=MESH)]
 
-    fetch(1, 2)
+    fetch(*range(1, NEAR))
+    for k in range(NEAR, layers):
+        ccopy(k).start()
     ins[0].wait()
     ins[1].wait()
     r, c = _iota((own, own), 0), _iota((own, own), 1)
@@ -118,13 +124,12 @@
     allr = own + hrows
     half = ch // 2
 
-    def gate(x, k):
+    def gate(x, k, z0):
         parts = []
         for q in range(2):
-            zf = jnp.dot(x, w1[k, :, q * half:(q + 1) * half], preferred_element_type=f32)
-            zg = jnp.dot(x, w1[k, :, ch + q * half:ch + (q + 1) * half], preferred_element_type=f32)
-            zf = zf + bias[k:k + 1, q * half:(q + 1) * half]
-            zg = zg + bias[k:k + 1, ch + q * half:ch + (q + 1) * half]
+            lo, hi = q * half, (q + 1) * half
+            zf = jnp.dot(x, w1[k, :, lo:hi], preferred_element_type=f32) + z0(lo, hi)
+            zg = jnp.dot(x, w1[k, :, ch + lo:ch + hi], preferred_element_type=f32) + z0(ch + lo, ch + hi)
             parts.append((jnp.tanh(zf) * (0.5 * jnp.tanh(0.5 * zg) + 0.5)).astype(bf16))
         return jnp.concatenate(parts, axis=1)
 
@@ -141,19 +146,21 @@
         hseq, hrho = (r - own) >> NEAR, (r - own) & (RES - 1)
         col = jnp.where(r < own, col, jnp.where(hrho >= d, own + hseq * RES + hrho - d, -1))
         p = jnp.dot((c == col).astype(bf16), u, preferred_element_type=f32).astype(bf16)
+        m = allr if k < NEAR - 1 else own
+        ccopy(k).wait()
+        zk = jnp.dot(call[:m], wc[k], preferred_element_type=f32) + bias[k:k + 1]
         for cp in wcopies(k):
             cp.wait()
-        a = gate(jnp.concatenate([u, p, call], axis=1), k)
-        dlt = jnp.dot(a, w2[k], preferred_element_type=f32)
+        a = gate(jnp.concatenate([u[:m], p[:m]], axis=1), k, lambda lo, hi: zk[:, lo:hi])
+        gates[k] = a[:own]
+        dlt = jnp.dot(a, w2[k, :, 0:ch], preferred_element_type=f32)
         if k == 0:
-            near[...] = dlt[:own, :ch]
-            s3[...] = dlt[:own, ch:]
+            near[...] = dlt[:own]
         else:
-            near[...] += dlt[:own, :ch]
-            s3[...] += dlt[:own, ch:]
-        h3[...] += dlt[:own, :ch]
+            near[...] += dlt[:own]
+        h3[...] += dlt[:own]
         if k < NEAR - 1:
-            halo_h = halo_h + dlt[own:, :ch]
+            halo_h = halo_h + dlt[own:]
 
     dsend[...] = near[...].reshape(n, chunks, per, ch).astype(TRAVEL)
     for ck in range(chunks):
@@ -166,18 +173,24 @@
             fetch(NEAR + 2, NEAR + 3)
 
     fetch(*range(NEAR + 4, layers))
+    skp = jnp.dot(gates[0], w2[0, :, ch:wide], preferred_element_type=f32)
+    for k in range(1, NEAR):
+        skp = skp + jnp.dot(gates[k], w2[k, :, ch:wide], preferred_element_type=f32)
+    s3[...] = skp
     drain(crecv, x_recv.at[chunks])
+    cq = jnp.concatenate([crecv[:, ck].astype(f32).reshape(rows, cch) for ck in range(chunks)], axis=0).astype(bf16)
+    for k in range(NEAR, layers):
+        ccopy(k).wait()
+        zc[k - NEAR] = jnp.dot(cq, wc[k], preferred_element_type=f32) + bias[k:k + 1]
+
     row = _iota((rows, ch), 0)
     for ck in range(chunks):
         drain(srecv.at[ck], x_recv.at[ck])
         drain(drecv.at[ck], d_recv.at[ck])
         base = (srecv[ck].astype(f32) + drecv[ck].astype(f32)).reshape(rows, ch)
-        cq = crecv[:, ck].astype(f32).reshape(rows, cch).astype(bf16)
-        h = base
+        h, a = base, None
         for k in range(NEAR, layers):
             sft = 2 ** (k - NEAR)
-            if k > NEAR:
-                h = base + far[:, 0:ch]
             if sft < 8:
                 past = jnp.where(row >= sft, pltpu.roll(h, sft, 0), 0.0)
             else:
@@ -185,14 +198,23 @@
             if ck == 0:
                 for cp in wcopies(k):
                     cp.wait()
-            a = gate(jnp.concatenate([h.astype(bf16), past.astype(bf16), cq], axis=1), k)
-            dlt = jnp.dot(a, w2[k], preferred_element_type=f32)
+            was, z_rows = a, slice(ck * rows, (ck + 1) * rows)
+            a = gate(jnp.concatenate([h.astype(bf16), past.astype(bf16)], axis=1), k,
+                     lambda lo, hi: zc[k - NEAR, z_rows, lo:hi])
+            if k == NEAR + 1:
+                far[:, ch:wide] = jnp.dot(was, w2[k - 1, :, ch:wide], preferred_element_type=f32)
+            elif k > NEAR + 1:
+                far[:, ch:wide] += jnp.dot(was, w2[k - 1, :, ch:wide], preferred_element_type=f32)
+            dlt = jnp.dot(a, w2[k, :, 0:ch], preferred_element_type=f32)
             if k == NEAR:
-                far[...] = dlt
+                far[:, 0:ch] = dlt
             elif k < layers - 1:
-                far[...] += dlt
-            else:
-                osend[ck] = (far[...] + dlt).reshape(n, per, wide).astype(TRAVEL)
+                far[:, 0:ch] += dlt
+            if k < layers - 1:
+                h = base + far[:, 0:ch]
+        osend[ck, :, :, 0:ch] = (far[:, 0:ch] + dlt).reshape(n, per, ch).astype(TRAVEL)
+        dlt = jnp.dot(a, w2[layers - 1, :, ch:wide], preferred_element_type=f32)
+        osend[ck, :, :, ch:wide] = (far[:, ch:wide] + dlt).reshape(n, per, wide - ch).astype(TRAVEL)
         for d in order:
             to = lax.rem(me + d, n)
             push(osend.at[ck, to], recv.at[ck, me], o_send, o_recv.at[ck], d, to)
@@ -253,8 +275,10 @@
             scratch_shapes=[
                 pltpu.VMEM((batch, span, ch), bf16), pltpu.VMEM((batch, span, cch), bf16),
                 pltpu.VMEM((batch, HALO, ch), bf16), pltpu.VMEM((batch, HALO, cch), bf16),
-                pltpu.VMEM((layers, 2 * ch + cch, 2 * ch), bf16), pltpu.VMEM((layers, ch, wide), bf16),
-                pltpu.VMEM((layers, 2 * ch), f32),
+                pltpu.VMEM((layers, 2 * ch, 2 * ch), bf16), pltpu.VMEM((layers, cch, 2 * ch), bf16),
+                pltpu.VMEM((layers, ch, wide), bf16),
+                pltpu.VMEM((layers, 2 * ch), f32), pltpu.VMEM((layers - NEAR, chunks * rows, 2 * ch), f32),
+                pltpu.VMEM((NEAR, own, ch), bf16),
                 pltpu.VMEM((own, ch), f32),
                 pltpu.VMEM((n, chunks, per, ch), bf16), pltpu.VMEM((n, chunks, per, cch), bf16),
                 pltpu.VMEM((n, chunks, per, ch), TRAVEL),

time: 43.7 us -> 45.3 us (1.037)
  Pallas kernels: 42.9 us -> 44.4 us
    pallas_call x1, Pallas kernels: 42 us -> 43.4 us  [local_stack(): pl.pallas_call(functools.partial(_stack, n), name='stack', out_shape=(plt...]
where the time goes in v7:
time: 45.3 us; the launch traced here: 45.2 us
  Pallas kernels  44.4 us (98%)
  between operations  0.8 us (2%)
    pallas_call x1, Pallas kernels, local_stack(): pl.pallas_call(functools.partial(_stack, n), name='stack', out_shape=(plt...  43.4 us
    pallas_call x1, Pallas kernels, local_stack(): pl.pallas_call(_finish, name='finish', out_shape=(sds((own, ch), f32), sd...  0.95 us

profile of v7, /device:TPU:21, one launch (start us, length us, event | category | flops | bytes accessed | tf_op | source)
XLA Modules:
  0.0 45.2 jit_solution(8408484166230084343)
XLA Ops:
  0.6 43.4 %stack.1 = (bf16[2,16,8,768]{3,2,1,0:T(8,128)(2,1)S(1)}, f32[256,512]{1,0:T(8,128)S(1)}, f32[256,256]{1,0:T(8,128)S(1)}) custom-call(bf16[4,64,512]{2,1,0:T(8,128)(2,1)} %sig_hbm.1, bf16[4,64,128]{2,1,0:T(8,128)(2,1)} %cond_hbm.1, bf16[10,512,1024]{2,1,0:T(8,128)(2,1)} %wn_hbm.1, bf16[10,512,1024]{2,1,0:T(8,128)(2,1)} %wp_hbm.1, ...), custom_call_target="tpu_custom_call" | custom-call | tf_op jit(solution)/shard_map/stack/pallas_call | solution.py:269
  44.1 1.0 %finish.1 = (f32[256,512]{1,0:T(8,128)}, f32[256,256]{1,0:T(8,128)}) custom-call(bf16[2,16,8,768]{3,2,1,0:T(8,128)(2,1)S(1)} %get-tuple-element.7.recv, f32[256,512]{1,0:T(8,128)S(1)} %get-tuple-element.8.h3, f32[256,256]{1,0:T(8,128)S(1)} %get-tuple-element.9.s3), custom_call_target="tpu_custom_call" | custom-call | tf_op jit(solution)/shard_map/finish/pallas_call | solution.py:294

commit v8 on v7

--- a/solution.py
+++ b/solution.py
@@ -22,7 +22,7 @@
 def _stack(n, sig_hbm, cond_hbm, wn_hbm, wp_hbm, wc_hbm, bg_hbm, wr_hbm, ws_hbm,
            recv, h3, s3,
            sig_v, cond_v, halo_s, halo_c, w1, wc, w2, bias, zc, gates,
-           near, ssend, csend, dsend, srecv, crecv, drecv, far, osend,
+           near, ssend, csend, dsend, srecv, crecv, drecv, osend,
            w_sem, in_sem, halo_send, halo_recv, x_send, x_recv, d_send, d_recv, o_send, o_recv):
     me = lax.axis_index("sp")
     batch, span, ch = sig_v.shape
@@ -77,13 +77,29 @@
         ccopy(k).start()
     ins[0].wait()
     ins[1].wait()
+    blk = rows + hrows // chunks
+    lg = (RES // chunks).bit_length() - 1
+
+    def place(r):
+        ck = (r >= blk).astype(jnp.int32)
+        rr = r - ck * blk
+        on_own = rr < rows
+        o = jnp.where(on_own, rr >> sh_per, rr - rows)
+        step = jnp.where(on_own, rr & (per - 1), -1)
+        return o >> lg, (o & ((1 << lg) - 1)) * chunks + ck, step
+
+    def row_of(seq, rho, step, one_chunk=False):
+        ck = 0 if one_chunk else rho & (chunks - 1)
+        o = seq * (1 << lg) + (rho >> (chunks.bit_length() - 1))
+        return ck * blk + jnp.where(step >= 0, o * per + step, rows + o)
+
     r, c = _iota((own, own), 0), _iota((own, own), 1)
-    seq, rho, step = r >> sh_span, (r >> sh_per) & (RES - 1), r & (per - 1)
+    seq, rho, step = place(r + hrows // chunks * (r >= rows).astype(jnp.int32))
     perm = (c == seq * span + step * RES + rho).astype(bf16)
     cnd = jnp.dot(perm, cond_v[...].reshape(own, cch), preferred_element_type=f32)
     sig = jnp.dot(perm, sig_v[...].reshape(own, ch), preferred_element_type=f32)
-    csend[...] = cnd.reshape(n, chunks, per, cch).astype(bf16)
-    ssend[...] = sig.reshape(n, chunks, per, ch).astype(bf16)
+    csend[...] = cnd.reshape(chunks, n, per, cch).astype(bf16)
+    ssend[...] = sig.reshape(chunks, n, per, ch).astype(bf16)
     h3[...] = sig
 
     pl.semaphore_wait(barrier, n - 1)
@@ -107,21 +123,25 @@
 
     for d in order:
         to = lax.rem(me + d, n)
-        push(csend.at[to], crecv.at[me], x_send.at[chunks], x_recv.at[chunks], d, to)
-        push(ssend.at[to, 0], srecv.at[0, me], x_send.at[0], x_recv.at[0], d, to)
+        push(csend.at[:, to], crecv.at[:, me], x_send.at[chunks], x_recv.at[chunks], d, to)
+        push(ssend.at[0, to], srecv.at[0, me], x_send.at[0], x_recv.at[0], d, to)
     fetch(NEAR, NEAR + 1)
 
     for cp in halo_copies():
         cp.wait_recv()
     ins[2].wait()
 
+    hh = hrows // chunks
     hr, hc = _iota((hrows, batch * HALO), 0), _iota((hrows, batch * HALO), 1)
-    pick = (hc == (hr >> NEAR) * HALO + (HALO - RES) + (hr & (RES - 1))).astype(bf16)
+    hck = (hr >= hh).astype(jnp.int32)
+    ho = hr - hck * hh
+    pick = (hc == (ho >> lg) * HALO + (HALO - RES) + (ho & ((1 << lg) - 1)) * chunks + hck).astype(bf16)
     live = me > 0
     halo_h = jnp.dot(pick, halo_s[...].reshape(batch * HALO, ch), preferred_element_type=f32)
     halo_k = jnp.dot(pick, halo_c[...].reshape(batch * HALO, cch), preferred_element_type=f32)
-    call = jnp.concatenate([cnd, halo_k], axis=0).astype(bf16)
-    allr = own + hrows
+    halo_h = jnp.where(live, halo_h, 0.0)
+    mix = lambda x, y: jnp.concatenate([x[:rows], y[:hh], x[rows:], y[hh:]], axis=0)
+    call = mix(cnd, halo_k).astype(bf16)
     half = ch // 2
 
     def gate(x, k, z0):
@@ -133,62 +153,79 @@
             parts.append((jnp.tanh(zf) * (0.5 * jnp.tanh(0.5 * zg) + 0.5)).astype(bf16))
         return jnp.concatenate(parts, axis=1)
 
-    for k in range(NEAR):
-        d = 2 ** k
-        u_halo = jnp.where(live, halo_h, 0.0)
-        u = jnp.concatenate([h3[...], u_halo], axis=0).astype(bf16)
-        r, c = _iota((allr, allr), 0), _iota((allr, allr), 1)
-        seq, rho, step = r >> sh_span, (r >> sh_per) & (RES - 1), r & (per - 1)
-        src = step * RES + rho - d
-        own_col = seq * span + ((src & (RES - 1)) << sh_per) + (src >> NEAR)
-        halo_col = own + seq * RES + src + RES
-        col = jnp.where(src >= 0, own_col, halo_col)
-        hseq, hrho = (r - own) >> NEAR, (r - own) & (RES - 1)
-        col = jnp.where(r < own, col, jnp.where(hrho >= d, own + hseq * RES + hrho - d, -1))
+    def narrow(a, w, lo, hi):
+        return [jnp.dot(a, w[:, c:min(c + 256, hi)], preferred_element_type=f32) for c in range(lo, hi, 256)]
+
+    def near_layer(k, h, cnd_rows, halo_out):
+        m = h.shape[0]
+        u = h.astype(bf16)
+        r, c = _iota((m, m), 0), _iota((m, m), 1)
+        seq, rho, step = place(r)
+        if m > blk:
+            src = step * RES + rho - 2 ** k
+            col = row_of(seq, src & (RES - 1), src >> NEAR)
+        else:
+            src = step * RES + rho - 2 ** k
+            col = row_of(seq, src & (RES - 1), src >> NEAR, True)
+        col = jnp.where(src >= -RES, col, -1)
         p = jnp.dot((c == col).astype(bf16), u, preferred_element_type=f32).astype(bf16)
-        m = allr if k < NEAR - 1 else own
-        ccopy(k).wait()
-        zk = jnp.dot(call[:m], wc[k], preferred_element_type=f32) + bias[k:k + 1]
-        for cp in wcopies(k):
-            cp.wait()
-        a = gate(jnp.concatenate([u[:m], p[:m]], axis=1), k, lambda lo, hi: zk[:, lo:hi])
-        gates[k] = a[:own]
-        dlt = jnp.dot(a, w2[k, :, 0:ch], preferred_element_type=f32)
-        if k == 0:
-            near[...] = dlt[:own]
-        else:
-            near[...] += dlt[:own]
-        h3[...] += dlt[:own]
-        if k < NEAR - 1:
-            halo_h = halo_h + dlt[own:]
-
-    dsend[...] = near[...].reshape(n, chunks, per, ch).astype(TRAVEL)
-    for ck in range(chunks):
+        keep = m if halo_out else rows
+        zk = jnp.dot(cnd_rows[:keep], wc[k], preferred_element_type=f32) + bias[k:k + 1]
+        a = gate(jnp.concatenate([u[:keep], p[:keep]], axis=1), k, lambda lo, hi: zk[:, lo:hi])
+        return a, jnp.concatenate(narrow(a, w2.at[k], 0, ch), axis=1)
+
+    ccopy(0).wait()
+    for cp in wcopies(0):
+        cp.wait()
+    h0 = mix(h3[...], halo_h)
+    a, d0 = near_layer(0, h0, call, True)
+    for ck in range(chunks):
+        gates[0, ck * rows:(ck + 1) * rows] = a[ck * blk:ck * blk + rows]
+    edge = (_iota((blk, ch), 0) < rows) | live
+    for ck in range(chunks):
+        part = slice(ck * blk, (ck + 1) * blk)
+        out = slice(ck * rows, (ck + 1) * rows)
+        acc = d0[part]
+        for k in range(1, NEAR):
+            if ck == 0:
+                ccopy(k).wait()
+                for cp in wcopies(k):
+                    cp.wait()
+            a, dk = near_layer(k, jnp.where(edge, h0[part] + acc, 0.0), call[part], k < NEAR - 1)
+            gates[k, out] = a[:rows]
+            acc = acc[:dk.shape[0]] + dk
+        dsend[ck] = acc.reshape(n, per, ch).astype(TRAVEL)
+        near[out] = acc
         for d in order:
             to = lax.rem(me + d, n)
             if ck > 0:
-                push(ssend.at[to, ck], srecv.at[ck, me], x_send.at[ck], x_recv.at[ck], d, to)
-            push(dsend.at[to, ck], drecv.at[ck, me], d_send, d_recv.at[ck], d, to)
+                push(ssend.at[ck, to], srecv.at[ck, me], x_send.at[ck], x_recv.at[ck], d, to)
+            push(dsend.at[ck, to], drecv.at[ck, me], d_send, d_recv.at[ck], d, to)
         if ck == 0:
             fetch(NEAR + 2, NEAR + 3)
-
     fetch(*range(NEAR + 4, layers))
+
     skp = jnp.dot(gates[0], w2[0, :, ch:wide], preferred_element_type=f32)
     for k in range(1, NEAR):
         skp = skp + jnp.dot(gates[k], w2[k, :, ch:wide], preferred_element_type=f32)
     s3[...] = skp
+    h3[...] += near[...]
     drain(crecv, x_recv.at[chunks])
-    cq = jnp.concatenate([crecv[:, ck].astype(f32).reshape(rows, cch) for ck in range(chunks)], axis=0).astype(bf16)
+    cq = jnp.concatenate([crecv[ck].astype(f32).reshape(rows, cch) for ck in range(chunks)], axis=0).astype(bf16)
     for k in range(NEAR, layers):
         ccopy(k).wait()
         zc[k - NEAR] = jnp.dot(cq, wc[k], preferred_element_type=f32) + bias[k:k + 1]
 
+    def late_skip(a, k):
+        return (jnp.dot(a[:, :half], w2[k, :half, ch:wide], preferred_element_type=f32)
+                + jnp.dot(a[:, half:], w2[k, half:, ch:wide], preferred_element_type=f32))
+
     row = _iota((rows, ch), 0)
     for ck in range(chunks):
         drain(srecv.at[ck], x_recv.at[ck])
         drain(drecv.at[ck], d_recv.at[ck])
         base = (srecv[ck].astype(f32) + drecv[ck].astype(f32)).reshape(rows, ch)
-        h, a = base, None
+        h, a, acc, skips = base, None, None, []
         for k in range(NEAR, layers):
             sft = 2 ** (k - NEAR)
             if sft < 8:
@@ -201,20 +238,14 @@
             was, z_rows = a, slice(ck * rows, (ck + 1) * rows)
             a = gate(jnp.concatenate([h.astype(bf16), past.astype(bf16)], axis=1), k,
                      lambda lo, hi: zc[k - NEAR, z_rows, lo:hi])
-            if k == NEAR + 1:
-                far[:, ch:wide] = jnp.dot(was, w2[k - 1, :, ch:wide], preferred_element_type=f32)
-            elif k > NEAR + 1:
-                far[:, ch:wide] += jnp.dot(was, w2[k - 1, :, ch:wide], preferred_element_type=f32)
-            dlt = jnp.dot(a, w2[k, :, 0:ch], preferred_element_type=f32)
-            if k == NEAR:
-                far[:, 0:ch] = dlt
-            elif k < layers - 1:
-                far[:, 0:ch] += dlt
-            if k < layers - 1:
-                h = base + far[:, 0:ch]
-        osend[ck, :, :, 0:ch] = (far[:, 0:ch] + dlt).reshape(n, per, ch).astype(TRAVEL)
-        dlt = jnp.dot(a, w2[layers - 1, :, ch:wide], preferred_element_type=f32)
-        osend[ck, :, :, ch:wide] = (far[:, ch:wide] + dlt).reshape(n, per, wide - ch).astype(TRAVEL)
+            if k > NEAR:
+                skips.append(late_skip(was, k - 1))
+            dlt = jnp.concatenate(narrow(a, w2.at[k], 0, ch), axis=1)
+            acc = dlt if k == NEAR else acc + dlt
+            h = base + acc
+        osend[ck, :, :, 0:ch] = acc.reshape(n, per, ch).astype(TRAVEL)
+        skips.append(late_skip(a, layers - 1))
+        osend[ck, :, :, ch:wide] = sum(skips[1:], skips[0]).reshape(n, per, wide - ch).astype(TRAVEL)
         for d in order:
             to = lax.rem(me + d, n)
             push(osend.at[ck, to], recv.at[ck, me], o_send, o_recv.at[ck], d, to)
@@ -222,8 +253,8 @@
     for cp in halo_copies():
         cp.wait_send()
     for ck in range(chunks):
-        drain(ssend.at[pl.ds(0, n - 1), ck], x_send.at[ck])
-    for buf, sem in ((csend.at[pl.ds(0, n - 1)], x_send.at[chunks]), (dsend.at[pl.ds(0, n - 1)], d_send), (osend.at[:, pl.ds(0, n - 1)], o_send)):
+        drain(ssend.at[ck, pl.ds(0, n - 1)], x_send.at[ck])
+    for buf, sem in ((csend.at[:, pl.ds(0, n - 1)], x_send.at[chunks]), (dsend.at[:, pl.ds(0, n - 1)], d_send), (osend.at[:, pl.ds(0, n - 1)], o_send)):
         drain(buf, sem)
     for ck in range(chunks):
         drain(recv.at[ck], o_recv.at[ck])
@@ -241,8 +272,9 @@
             for j in range(n):
                 cl = j * chunks + ck
                 s, rho = cl // RES, cl % RES
+                at = (ck * n + j) * per
                 obuf[t, pl.ds(s * span + rho, per, RES), :] = (
-                    recv[ck, j, :, lo:lo + 128].astype(f32) + base[cl * per:(cl + 1) * per, off:off + 128])
+                    recv[ck, j, :, lo:lo + 128].astype(f32) + base[at:at + per, off:off + 128])
         dst = hout_hbm if lo < ch else sout_hbm
         outs.append(pltpu.make_async_copy(obuf.at[t], dst.at[:, pl.ds(off, 128)], out_sem.at[t]))
         outs[-1].start()
@@ -280,11 +312,11 @@
                 pltpu.VMEM((layers, 2 * ch), f32), pltpu.VMEM((layers - NEAR, chunks * rows, 2 * ch), f32),
                 pltpu.VMEM((NEAR, own, ch), bf16),
                 pltpu.VMEM((own, ch), f32),
-                pltpu.VMEM((n, chunks, per, ch), bf16), pltpu.VMEM((n, chunks, per, cch), bf16),
-                pltpu.VMEM((n, chunks, per, ch), TRAVEL),
-                pltpu.VMEM((chunks, n, per, ch), bf16), pltpu.VMEM((n, chunks, per, cch), bf16),
+                pltpu.VMEM((chunks, n, per, ch), bf16), pltpu.VMEM((chunks, n, per, cch), bf16),
                 pltpu.VMEM((chunks, n, per, ch), TRAVEL),
-                pltpu.VMEM((rows, wide), f32), pltpu.VMEM((chunks, n, per, wide), TRAVEL),
+                pltpu.VMEM((chunks, n, per, ch), bf16), pltpu.VMEM((chunks, n, per, cch), bf16),
+                pltpu.VMEM((chunks, n, per, ch), TRAVEL),
+                pltpu.VMEM((chunks, n, per, wide), TRAVEL),
                 dma((layers, 5)), dma((3,)), dma((2,)), dma((2,)), dma((chunks + 1,)), dma((chunks + 1,)),
                 dma, dma((chunks,)), dma, dma((chunks,)),
             ],

time: 45.3 us -> 43.4 us (0.958)
  Pallas kernels: 44.4 us -> 42.5 us
    pallas_call x1, Pallas kernels: 43.4 us -> 41.6 us  [local_stack(): pl.pallas_call(functools.partial(_stack, n), name='stack', out_shape=(plt...]
where the time goes in v8:
time: 43.4 us; the launch traced here: 43.3 us
  Pallas kernels  42.5 us (98%)
  between operations  0.8 us (2%)
    pallas_call x1, Pallas kernels, local_stack(): pl.pallas_call(functools.partial(_stack, n), name='stack', out_shape=(plt...  41.6 us
    pallas_call x1, Pallas kernels, local_stack(): pl.pallas_call(_finish, name='finish', out_shape=(sds((own, ch), f32), sd...  0.95 us

profile of v8, /device:TPU:21, one launch (start us, length us, event | category | flops | bytes accessed | tf_op | source)
XLA Modules:
  0.0 43.3 jit_solution(16380597713230445369)
XLA Ops:
  0.6 41.6 %stack.1 = (bf16[2,16,8,768]{3,2,1,0:T(8,128)(2,1)S(1)}, f32[256,512]{1,0:T(8,128)S(1)}, f32[256,256]{1,0:T(8,128)S(1)}) custom-call(bf16[4,64,512]{2,1,0:T(8,128)(2,1)} %sig_hbm.1, bf16[4,64,128]{2,1,0:T(8,128)(2,1)} %cond_hbm.1, bf16[10,512,1024]{2,1,0:T(8,128)(2,1)} %wn_hbm.1, bf16[10,512,1024]{2,1,0:T(8,128)(2,1)} %wp_hbm.1, ...), custom_call_target="tpu_custom_call" | custom-call | tf_op jit(solution)/shard_map/stack/pallas_call | solution.py:301
  42.2 1.0 %finish.1 = (f32[256,512]{1,0:T(8,128)}, f32[256,256]{1,0:T(8,128)}) custom-call(bf16[2,16,8,768]{3,2,1,0:T(8,128)(2,1)S(1)} %get-tuple-element.7.recv, f32[256,512]{1,0:T(8,128)S(1)} %get-tuple-element.8.h3, f32[256,256]{1,0:T(8,128)S(1)} %get-tuple-element.9.s3), custom_call_target="tpu_custom_call" | custom-call | tf_op jit(solution)/shard_map/finish/pallas_call | solution.py:326

commit v9 on v8

--- a/solution.py
+++ b/solution.py
@@ -12,6 +12,7 @@
 RES = 2 ** NEAR
 HALO = 16
 f32, bf16 = jnp.float32, jnp.bfloat16
+LEAD = 3
 TRAVEL = bf16
 
 
@@ -123,8 +124,8 @@
 
     for d in order:
         to = lax.rem(me + d, n)
-        push(csend.at[:, to], crecv.at[:, me], x_send.at[chunks], x_recv.at[chunks], d, to)
-        push(ssend.at[0, to], srecv.at[0, me], x_send.at[0], x_recv.at[0], d, to)
+        push(ssend.at[:, to], srecv.at[:, me], x_send.at[0], x_recv.at[0], d, to)
+        push(csend.at[:, to], crecv.at[:, me], x_send.at[1], x_recv.at[1], d, to)
     fetch(NEAR, NEAR + 1)
 
     for cp in halo_copies():
@@ -198,8 +199,6 @@
         near[out] = acc
         for d in order:
             to = lax.rem(me + d, n)
-            if ck > 0:
-                push(ssend.at[ck, to], srecv.at[ck, me], x_send.at[ck], x_recv.at[ck], d, to)
             push(dsend.at[ck, to], drecv.at[ck, me], d_send, d_recv.at[ck], d, to)
         if ck == 0:
             fetch(NEAR + 2, NEAR + 3)
@@ -210,7 +209,7 @@
         skp = skp + jnp.dot(gates[k], w2[k, :, ch:wide], preferred_element_type=f32)
     s3[...] = skp
     h3[...] += near[...]
-    drain(crecv, x_recv.at[chunks])
+    drain(crecv, x_recv.at[1])
     cq = jnp.concatenate([crecv[ck].astype(f32).reshape(rows, cch) for ck in range(chunks)], axis=0).astype(bf16)
     for k in range(NEAR, layers):
         ccopy(k).wait()
@@ -221,40 +220,59 @@
                 + jnp.dot(a[:, half:], w2[k, half:, ch:wide], preferred_element_type=f32))
 
     row = _iota((rows, ch), 0)
-    for ck in range(chunks):
-        drain(srecv.at[ck], x_recv.at[ck])
+    drain(srecv, x_recv.at[0])
+    base, acc, act, skips = [None] * chunks, [None] * chunks, [None] * chunks, [[] for _ in range(chunks)]
+
+    def begin(ck):
         drain(drecv.at[ck], d_recv.at[ck])
-        base = (srecv[ck].astype(f32) + drecv[ck].astype(f32)).reshape(rows, ch)
-        h, a, acc, skips = base, None, None, []
-        for k in range(NEAR, layers):
-            sft = 2 ** (k - NEAR)
-            if sft < 8:
-                past = jnp.where(row >= sft, pltpu.roll(h, sft, 0), 0.0)
-            else:
-                past = jnp.concatenate([jnp.zeros((sft, ch), f32), h[:rows - sft]], axis=0)
-            if ck == 0:
-                for cp in wcopies(k):
-                    cp.wait()
-            was, z_rows = a, slice(ck * rows, (ck + 1) * rows)
-            a = gate(jnp.concatenate([h.astype(bf16), past.astype(bf16)], axis=1), k,
-                     lambda lo, hi: zc[k - NEAR, z_rows, lo:hi])
-            if k > NEAR:
-                skips.append(late_skip(was, k - 1))
-            dlt = jnp.concatenate(narrow(a, w2.at[k], 0, ch), axis=1)
-            acc = dlt if k == NEAR else acc + dlt
-            h = base + acc
-        osend[ck, :, :, 0:ch] = acc.reshape(n, per, ch).astype(TRAVEL)
-        skips.append(late_skip(a, layers - 1))
-        osend[ck, :, :, ch:wide] = sum(skips[1:], skips[0]).reshape(n, per, wide - ch).astype(TRAVEL)
+        base[ck] = (srecv[ck].astype(f32) + drecv[ck].astype(f32)).reshape(rows, ch)
+
+    def first_half(ck, k):
+        h = base[ck] if k == NEAR else base[ck] + acc[ck]
+        sft = 2 ** (k - NEAR)
+        if sft < 8:
+            past = jnp.where(row >= sft, pltpu.roll(h, sft, 0), 0.0)
+        else:
+            past = jnp.concatenate([jnp.zeros((sft, ch), f32), h[:rows - sft]], axis=0)
+        if ck == 0:
+            for cp in wcopies(k):
+                cp.wait()
+        z_rows = slice(ck * rows, (ck + 1) * rows)
+        return gate(jnp.concatenate([h.astype(bf16), past.astype(bf16)], axis=1), k,
+                    lambda lo, hi: zc[k - NEAR, z_rows, lo:hi])
+
+    def second_half(ck, k, a):
+        if k > NEAR:
+            skips[ck].append(late_skip(act[ck], k - 1))
+        act[ck] = a
+        dlt = jnp.concatenate(narrow(a, w2.at[k], 0, ch), axis=1)
+        acc[ck] = dlt if k == NEAR else acc[ck] + dlt
+
+    def send_back(ck):
+        osend[ck, :, :, 0:ch] = acc[ck].reshape(n, per, ch).astype(TRAVEL)
+        skips[ck].append(late_skip(act[ck], layers - 1))
+        osend[ck, :, :, ch:wide] = sum(skips[ck][1:], skips[ck][0]).reshape(n, per, wide - ch).astype(TRAVEL)
         for d in order:
             to = lax.rem(me + d, n)
             push(osend.at[ck, to], recv.at[ck, me], o_send, o_recv.at[ck], d, to)
 
+    begin(0)
+    for k in range(NEAR, NEAR + LEAD):
+        second_half(0, k, first_half(0, k))
+    begin(1)
+    for k in range(NEAR + LEAD, layers):
+        a0 = first_half(0, k)
+        a1 = first_half(1, k - LEAD)
+        second_half(0, k, a0)
+        second_half(1, k - LEAD, a1)
+    send_back(0)
+    for k in range(layers - LEAD, layers):
+        second_half(1, k, first_half(1, k))
+    send_back(1)
+
     for cp in halo_copies():
         cp.wait_send()
-    for ck in range(chunks):
-        drain(ssend.at[ck, pl.ds(0, n - 1)], x_send.at[ck])
-    for buf, sem in ((csend.at[:, pl.ds(0, n - 1)], x_send.at[chunks]), (dsend.at[:, pl.ds(0, n - 1)], d_send), (osend.at[:, pl.ds(0, n - 1)], o_send)):
+    for buf, sem in ((ssend.at[:, pl.ds(0, n - 1)], x_send.at[0]), (csend.at[:, pl.ds(0, n - 1)], x_send.at[1]), (dsend.at[:, pl.ds(0, n - 1)], d_send), (osend.at[:, pl.ds(0, n - 1)], o_send)):
         drain(buf, sem)
     for ck in range(chunks):
         drain(recv.at[ck], o_recv.at[ck])
@@ -317,7 +335,7 @@
                 pltpu.VMEM((chunks, n, per, ch), bf16), pltpu.VMEM((chunks, n, per, cch), bf16),
                 pltpu.VMEM((chunks, n, per, ch), TRAVEL),
                 pltpu.VMEM((chunks, n, per, wide), TRAVEL),
-                dma((layers, 5)), dma((3,)), dma((2,)), dma((2,)), dma((chunks + 1,)), dma((chunks + 1,)),
+                dma((layers, 5)), dma((3,)), dma((2,)), dma((2,)), dma((2,)), dma((2,)),
                 dma, dma((chunks,)), dma, dma((chunks,)),
             ],
             compiler_params=pltpu.CompilerParams(collective_id=0, has_side_effects=True,

time: 43.4 us -> 45 us (1.037)
  Pallas kernels: 42.5 us -> 44.3 us
    pallas_call x1, Pallas kernels: 41.6 us -> 43.3 us  [local_stack(): pl.pallas_call(functools.partial(_stack, n), name='stack', out_shape=(plt...]
where the time goes in v9:
time: 45 us; the launch traced here: 44.9 us
  Pallas kernels  44.3 us (98%)
  between operations  0.64 us (1%)
    pallas_call x1, Pallas kernels, local_stack(): pl.pallas_call(functools.partial(_stack, n), name='stack', out_shape=(plt...  43.3 us
    pallas_call x1, Pallas kernels, local_stack(): pl.pallas_call(_finish, name='finish', out_shape=(sds((own, ch), f32), sd...  0.95 us

profile of v9, /device:TPU:21, one launch (start us, length us, event | category | flops | bytes accessed | tf_op | source)
XLA Modules:
  0.0 44.9 jit_solution(14647436902487337153)
XLA Ops:
  0.6 43.3 %stack.1 = (bf16[2,16,8,768]{3,2,1,0:T(8,128)(2,1)S(1)}, f32[256,512]{1,0:T(8,128)S(1)}, f32[256,256]{1,0:T(8,128)S(1)}) custom-call(bf16[4,64,512]{2,1,0:T(8,128)(2,1)} %sig_hbm.1, bf16[4,64,128]{2,1,0:T(8,128)(2,1)} %cond_hbm.1, bf16[10,512,1024]{2,1,0:T(8,128)(2,1)} %wn_hbm.1, bf16[10,512,1024]{2,1,0:T(8,128)(2,1)} %wp_hbm.1, ...), custom_call_target="tpu_custom_call" | custom-call | tf_op jit(solution)/shard_map/stack/pallas_call | solution.py:319
  44.0 1.0 %finish.1 = (f32[256,512]{1,0:T(8,128)}, f32[256,256]{1,0:T(8,128)}) custom-call(bf16[2,16,8,768]{3,2,1,0:T(8,128)(2,1)S(1)} %get-tuple-element.7.recv, f32[256,512]{1,0:T(8,128)S(1)} %get-tuple-element.8.h3, f32[256,256]{1,0:T(8,128)S(1)} %get-tuple-element.9.s3), custom_call_target="tpu_custom_call" | custom-call | tf_op jit(solution)/shard_map/finish/pallas_call | solution.py:344

commit v10 on v9

--- a/solution.py
+++ b/solution.py
@@ -12,7 +12,7 @@
 RES = 2 ** NEAR
 HALO = 16
 f32, bf16 = jnp.float32, jnp.bfloat16
-LEAD = 3
+LEAD = 7
 TRAVEL = bf16
 
 

time: 45 us -> 44.2 us (0.982)
  Pallas kernels: 44.3 us -> 43.4 us
    pallas_call x1, Pallas kernels: 43.3 us -> 42.4 us  [local_stack(): pl.pallas_call(functools.partial(_stack, n), name='stack', out_shape=(plt...]
where the time goes in v10:
time: 44.2 us
  Pallas kernels  43.4 us (98%)
  between operations  0.8 us (2%)
    pallas_call x1, Pallas kernels, local_stack(): pl.pallas_call(functools.partial(_stack, n), name='stack', out_shape=(plt...  42.4 us
    pallas_call x1, Pallas kernels, local_stack(): pl.pallas_call(_finish, name='finish', out_shape=(sds((own, ch), f32), sd...  0.95 us

profile of v10, /device:TPU:21, one launch (start us, length us, event | category | flops | bytes accessed | tf_op | source)
XLA Modules:
  0.0 44.2 jit_solution(14977792886498712597)
XLA Ops:
  0.6 42.4 %stack.1 = (bf16[2,16,8,768]{3,2,1,0:T(8,128)(2,1)S(1)}, f32[256,512]{1,0:T(8,128)S(1)}, f32[256,256]{1,0:T(8,128)S(1)}) custom-call(bf16[4,64,512]{2,1,0:T(8,128)(2,1)} %sig_hbm.1, bf16[4,64,128]{2,1,0:T(8,128)(2,1)} %cond_hbm.1, bf16[10,512,1024]{2,1,0:T(8,128)(2,1)} %wn_hbm.1, bf16[10,512,1024]{2,1,0:T(8,128)(2,1)} %wp_hbm.1, ...), custom_call_target="tpu_custom_call" | custom-call | tf_op jit(solution)/shard_map/stack/pallas_call | solution.py:319
  43.1 1.0 %finish.1 = (f32[256,512]{1,0:T(8,128)}, f32[256,256]{1,0:T(8,128)}) custom-call(bf16[2,16,8,768]{3,2,1,0:T(8,128)(2,1)S(1)} %get-tuple-element.7.recv, f32[256,512]{1,0:T(8,128)S(1)} %get-tuple-element.8.h3, f32[256,256]{1,0:T(8,128)S(1)} %get-tuple-element.9.s3), custom_call_target="tpu_custom_call" | custom-call | tf_op jit(solution)/shard_map/finish/pallas_call | solution.py:344

commit v11 on v8

--- a/solution.py
+++ b/solution.py
@@ -21,8 +21,8 @@
 
 def _stack(n, sig_hbm, cond_hbm, wn_hbm, wp_hbm, wc_hbm, bg_hbm, wr_hbm, ws_hbm,
            recv, h3, s3,
-           sig_v, cond_v, halo_s, halo_c, w1, wc, w2, bias, zc, gates,
-           near, ssend, csend, dsend, srecv, crecv, drecv, osend,
+           sig_v, cond_v, halo_s, halo_c, w1, w2, bias, gates,
+           near, ssend, csend, dsend, srecv, crecv, drecv, far, osend,
            w_sem, in_sem, halo_send, halo_recv, x_send, x_recv, d_send, d_recv, o_send, o_recv):
     me = lax.axis_index("sp")
     batch, span, ch = sig_v.shape
@@ -50,19 +50,15 @@
     def wcopies(k):
         return [pltpu.make_async_copy(wn_hbm.at[k], w1.at[k, pl.ds(0, ch)], w_sem.at[k, 0]),
                 pltpu.make_async_copy(wp_hbm.at[k], w1.at[k, pl.ds(ch, ch)], w_sem.at[k, 1]),
-                pltpu.make_async_copy(wr_hbm.at[k], w2.at[k, :, pl.ds(0, ch)], w_sem.at[k, 2]),
-                pltpu.make_async_copy(ws_hbm.at[k], w2.at[k, :, pl.ds(ch, wide - ch)], w_sem.at[k, 3])]
-
-    def ccopy(k):
-        return pltpu.make_async_copy(wc_hbm.at[k], wc.at[k], w_sem.at[k, 4])
+                pltpu.make_async_copy(wc_hbm.at[k], w1.at[k, pl.ds(2 * ch, cch)], w_sem.at[k, 2]),
+                pltpu.make_async_copy(wr_hbm.at[k], w2.at[k, :, pl.ds(0, ch)], w_sem.at[k, 3]),
+                pltpu.make_async_copy(ws_hbm.at[k], w2.at[k, :, pl.ds(ch, wide - ch)], w_sem.at[k, 4])]
 
     def fetch(*ks):
         for k in ks:
             for c in wcopies(k):
                 c.start()
 
-    for k in range(NEAR):
-        ccopy(k).start()
     fetch(0)
 
     def halo_copies():
@@ -73,8 +69,6 @@
                                              halo_recv.at[1], device_id={"sp": nxt}, device_id_type=MESH)]
 
     fetch(*range(1, NEAR))
-    for k in range(NEAR, layers):
-        ccopy(k).start()
     ins[0].wait()
     ins[1].wait()
     blk = rows + hrows // chunks
@@ -144,17 +138,14 @@
     call = mix(cnd, halo_k).astype(bf16)
     half = ch // 2
 
-    def gate(x, k, z0):
+    def gate(x, k):
         parts = []
         for q in range(2):
             lo, hi = q * half, (q + 1) * half
-            zf = jnp.dot(x, w1[k, :, lo:hi], preferred_element_type=f32) + z0(lo, hi)
-            zg = jnp.dot(x, w1[k, :, ch + lo:ch + hi], preferred_element_type=f32) + z0(ch + lo, ch + hi)
+            zf = jnp.dot(x, w1[k, :, lo:hi], preferred_element_type=f32) + bias[k:k + 1, lo:hi]
+            zg = jnp.dot(x, w1[k, :, ch + lo:ch + hi], preferred_element_type=f32) + bias[k:k + 1, ch + lo:ch + hi]
             parts.append((jnp.tanh(zf) * (0.5 * jnp.tanh(0.5 * zg) + 0.5)).astype(bf16))
         return jnp.concatenate(parts, axis=1)
-
-    def narrow(a, w, lo, hi):
-        return [jnp.dot(a, w[:, c:min(c + 256, hi)], preferred_element_type=f32) for c in range(lo, hi, 256)]
 
     def near_layer(k, h, cnd_rows, halo_out):
         m = h.shape[0]
@@ -170,11 +161,9 @@
         col = jnp.where(src >= -RES, col, -1)
         p = jnp.dot((c == col).astype(bf16), u, preferred_element_type=f32).astype(bf16)
         keep = m if halo_out else rows
-        zk = jnp.dot(cnd_rows[:keep], wc[k], preferred_element_type=f32) + bias[k:k + 1]
-        a = gate(jnp.concatenate([u[:keep], p[:keep]], axis=1), k, lambda lo, hi: zk[:, lo:hi])
-        return a, jnp.concatenate(narrow(a, w2.at[k], 0, ch), axis=1)
-
-    ccopy(0).wait()
+        a = gate(jnp.concatenate([u[:keep], p[:keep], cnd_rows[:keep]], axis=1), k)
+        return a, jnp.dot(a, w2[k, :, 0:ch], preferred_element_type=f32)
+
     for cp in wcopies(0):
         cp.wait()
     h0 = mix(h3[...], halo_h)
@@ -188,7 +177,6 @@
         acc = d0[part]
         for k in range(1, NEAR):
             if ck == 0:
-                ccopy(k).wait()
                 for cp in wcopies(k):
                     cp.wait()
             a, dk = near_layer(k, jnp.where(edge, h0[part] + acc, 0.0), call[part], k < NEAR - 1)
@@ -211,23 +199,17 @@
     s3[...] = skp
     h3[...] += near[...]
     drain(crecv, x_recv.at[chunks])
-    cq = jnp.concatenate([crecv[ck].astype(f32).reshape(rows, cch) for ck in range(chunks)], axis=0).astype(bf16)
-    for k in range(NEAR, layers):
-        ccopy(k).wait()
-        zc[k - NEAR] = jnp.dot(cq, wc[k], preferred_element_type=f32) + bias[k:k + 1]
-
-    def late_skip(a, k):
-        return (jnp.dot(a[:, :half], w2[k, :half, ch:wide], preferred_element_type=f32)
-                + jnp.dot(a[:, half:], w2[k, half:, ch:wide], preferred_element_type=f32))
-
     row = _iota((rows, ch), 0)
     for ck in range(chunks):
         drain(srecv.at[ck], x_recv.at[ck])
         drain(drecv.at[ck], d_recv.at[ck])
         base = (srecv[ck].astype(f32) + drecv[ck].astype(f32)).reshape(rows, ch)
-        h, a, acc, skips = base, None, None, []
+        cq = crecv[ck].astype(f32).reshape(rows, cch).astype(bf16)
+        h = base
         for k in range(NEAR, layers):
             sft = 2 ** (k - NEAR)
+            if k > NEAR:
+                h = base + far[:, 0:ch]
             if sft < 8:
                 past = jnp.where(row >= sft, pltpu.roll(h, sft, 0), 0.0)
             else:
@@ -235,17 +217,14 @@
             if ck == 0:
                 for cp in wcopies(k):
                     cp.wait()
-            was, z_rows = a, slice(ck * rows, (ck + 1) * rows)
-            a = gate(jnp.concatenate([h.astype(bf16), past.astype(bf16)], axis=1), k,
-                     lambda lo, hi: zc[k - NEAR, z_rows, lo:hi])
-            if k > NEAR:
-                skips.append(late_skip(was, k - 1))
-            dlt = jnp.concatenate(narrow(a, w2.at[k], 0, ch), axis=1)
-            acc = dlt if k == NEAR else acc + dlt
-            h = base + acc
-        osend[ck, :, :, 0:ch] = acc.reshape(n, per, ch).astype(TRAVEL)
-        skips.append(late_skip(a, layers - 1))
-        osend[ck, :, :, ch:wide] = sum(skips[1:], skips[0]).reshape(n, per, wide - ch).astype(TRAVEL)
+            a = gate(jnp.concatenate([h.astype(bf16), past.astype(bf16), cq], axis=1), k)
+            dlt = jnp.dot(a, w2[k], preferred_element_type=f32)
+            if k == NEAR:
+                far[...] = dlt
+            elif k < layers - 1:
+                far[...] += dlt
+            else:
+                osend[ck] = (far[...] + dlt).reshape(n, per, wide).astype(TRAVEL)
         for d in order:
             to = lax.rem(me + d, n)
             push(osend.at[ck, to], recv.at[ck, me], o_send, o_recv.at[ck], d, to)
@@ -307,16 +286,15 @@
             scratch_shapes=[
                 pltpu.VMEM((batch, span, ch), bf16), pltpu.VMEM((batch, span, cch), bf16),
                 pltpu.VMEM((batch, HALO, ch), bf16), pltpu.VMEM((batch, HALO, cch), bf16),
-                pltpu.VMEM((layers, 2 * ch, 2 * ch), bf16), pltpu.VMEM((layers, cch, 2 * ch), bf16),
-                pltpu.VMEM((layers, ch, wide), bf16),
-                pltpu.VMEM((layers, 2 * ch), f32), pltpu.VMEM((layers - NEAR, chunks * rows, 2 * ch), f32),
+                pltpu.VMEM((layers, 2 * ch + cch, 2 * ch), bf16), pltpu.VMEM((layers, ch, wide), bf16),
+                pltpu.VMEM((layers, 2 * ch), f32),
                 pltpu.VMEM((NEAR, own, ch), bf16),
                 pltpu.VMEM((own, ch), f32),
                 pltpu.VMEM((chunks, n, per, ch), bf16), pltpu.VMEM((chunks, n, per, cch), bf16),
                 pltpu.VMEM((chunks, n, per, ch), TRAVEL),
                 pltpu.VMEM((chunks, n, per, ch), bf16), pltpu.VMEM((chunks, n, per, cch), bf16),
                 pltpu.VMEM((chunks, n, per, ch), TRAVEL),
-                pltpu.VMEM((chunks, n, per, wide), TRAVEL),
+                pltpu.VMEM((rows, wide), f32), pltpu.VMEM((chunks, n, per, wide), TRAVEL),
                 dma((layers, 5)), dma((3,)), dma((2,)), dma((2,)), dma((chunks + 1,)), dma((chunks + 1,)),
                 dma, dma((chunks,)), dma, dma((chunks,)),
             ],

time: 43.4 us -> 42.5 us (0.979)
  Pallas kernels: 42.5 us -> 41.6 us
    pallas_call x1, Pallas kernels: 41.6 us -> 40.6 us  [local_stack(): pl.pallas_call(functools.partial(_stack, n), name='stack', out_shape=(plt...]
where the time goes in v11:
time: 42.5 us; the launch traced here: 42.4 us
  Pallas kernels  41.6 us (98%)
  between operations  0.8 us (2%)
    pallas_call x1, Pallas kernels, local_stack(): pl.pallas_call(functools.partial(_stack, n), name='stack', out_shape=(plt...  40.6 us
    pallas_call x1, Pallas kernels, local_stack(): pl.pallas_call(_finish, name='finish', out_shape=(sds((own, ch), f32), sd...  0.95 us

profile of v11, /device:TPU:21, one launch (start us, length us, event | category | flops | bytes accessed | tf_op | source)
XLA Modules:
  0.0 42.4 jit_solution(16034185165252365497)
XLA Ops:
  0.6 40.6 %stack.1 = (bf16[2,16,8,768]{3,2,1,0:T(8,128)(2,1)S(1)}, f32[256,512]{1,0:T(8,128)S(1)}, f32[256,256]{1,0:T(8,128)S(1)}) custom-call(bf16[4,64,512]{2,1,0:T(8,128)(2,1)} %sig_hbm.1, bf16[4,64,128]{2,1,0:T(8,128)(2,1)} %cond_hbm.1, bf16[10,512,1024]{2,1,0:T(8,128)(2,1)} %wn_hbm.1, bf16[10,512,1024]{2,1,0:T(8,128)(2,1)} %wp_hbm.1, ...), custom_call_target="tpu_custom_call" | custom-call | tf_op jit(solution)/shard_map/stack/pallas_call | solution.py:280
  41.3 1.0 %finish.1 = (f32[256,512]{1,0:T(8,128)}, f32[256,256]{1,0:T(8,128)}) custom-call(bf16[2,16,8,768]{3,2,1,0:T(8,128)(2,1)S(1)} %get-tuple-element.7.recv, f32[256,512]{1,0:T(8,128)S(1)} %get-tuple-element.8.h3, f32[256,256]{1,0:T(8,128)S(1)} %get-tuple-element.9.s3), custom_call_target="tpu_custom_call" | custom-call | tf_op jit(solution)/shard_map/finish/pallas_call | solution.py:304

commit v12 on v11

--- a/solution.py
+++ b/solution.py
@@ -68,7 +68,6 @@
                 pltpu.make_async_remote_copy(cond_v.at[:, pl.ds(span - HALO, HALO)], halo_c, halo_send.at[1],
                                              halo_recv.at[1], device_id={"sp": nxt}, device_id_type=MESH)]
 
-    fetch(*range(1, NEAR))
     ins[0].wait()
     ins[1].wait()
     blk = rows + hrows // chunks
@@ -119,7 +118,7 @@
         to = lax.rem(me + d, n)
         push(csend.at[:, to], crecv.at[:, me], x_send.at[chunks], x_recv.at[chunks], d, to)
         push(ssend.at[0, to], srecv.at[0, me], x_send.at[0], x_recv.at[0], d, to)
-    fetch(NEAR, NEAR + 1)
+    fetch(*range(1, NEAR + 2))
 
     for cp in halo_copies():
         cp.wait_recv()

time: 42.5 us -> 42 us (0.988)
  Pallas kernels: 41.6 us -> 41.1 us
    pallas_call x1, Pallas kernels: 40.6 us -> 40.1 us  [local_stack(): pl.pallas_call(functools.partial(_stack, n), name='stack', out_shape=(plt...]
where the time goes in v12:
time: 42 us; the launch traced here: 41.9 us
  Pallas kernels  41.1 us (98%)
  between operations  0.8 us (2%)
    pallas_call x1, Pallas kernels, local_stack(): pl.pallas_call(functools.partial(_stack, n), name='stack', out_shape=(plt...  40.1 us
    pallas_call x1, Pallas kernels, local_stack(): pl.pallas_call(_finish, name='finish', out_shape=(sds((own, ch), f32), sd...  0.95 us

profile of v12, /device:TPU:21, one launch (start us, length us, event | category | flops | bytes accessed | tf_op | source)
XLA Modules:
  0.0 41.9 jit_solution(16714008729692119464)
XLA Ops:
  0.6 40.1 %stack.1 = (bf16[2,16,8,768]{3,2,1,0:T(8,128)(2,1)S(1)}, f32[256,512]{1,0:T(8,128)S(1)}, f32[256,256]{1,0:T(8,128)S(1)}) custom-call(bf16[4,64,512]{2,1,0:T(8,128)(2,1)} %sig_hbm.1, bf16[4,64,128]{2,1,0:T(8,128)(2,1)} %cond_hbm.1, bf16[10,512,1024]{2,1,0:T(8,128)(2,1)} %wn_hbm.1, bf16[10,512,1024]{2,1,0:T(8,128)(2,1)} %wp_hbm.1, ...), custom_call_target="tpu_custom_call" | custom-call | tf_op jit(solution)/shard_map/stack/pallas_call | solution.py:279
  40.8 1.0 %finish.1 = (f32[256,512]{1,0:T(8,128)}, f32[256,256]{1,0:T(8,128)}) custom-call(bf16[2,16,8,768]{3,2,1,0:T(8,128)(2,1)S(1)} %get-tuple-element.7.recv, f32[256,512]{1,0:T(8,128)S(1)} %get-tuple-element.8.h3, f32[256,256]{1,0:T(8,128)S(1)} %get-tuple-element.9.s3), custom_call_target="tpu_custom_call" | custom-call | tf_op jit(solution)/shard_map/finish/pallas_call | solution.py:303

commit v13 on v12

--- a/solution.py
+++ b/solution.py
@@ -22,7 +22,7 @@
 def _stack(n, sig_hbm, cond_hbm, wn_hbm, wp_hbm, wc_hbm, bg_hbm, wr_hbm, ws_hbm,
            recv, h3, s3,
            sig_v, cond_v, halo_s, halo_c, w1, w2, bias, gates,
-           near, ssend, csend, dsend, srecv, crecv, drecv, far, osend,
+           near, xsend, dsend, bsend, xrecv, drecv, brecv, far, osend,
            w_sem, in_sem, halo_send, halo_recv, x_send, x_recv, d_send, d_recv, o_send, o_recv):
     me = lax.axis_index("sp")
     batch, span, ch = sig_v.shape
@@ -91,8 +91,13 @@
     perm = (c == seq * span + step * RES + rho).astype(bf16)
     cnd = jnp.dot(perm, cond_v[...].reshape(own, cch), preferred_element_type=f32)
     sig = jnp.dot(perm, sig_v[...].reshape(own, ch), preferred_element_type=f32)
-    csend[...] = cnd.reshape(chunks, n, per, cch).astype(bf16)
-    ssend[...] = sig.reshape(chunks, n, per, ch).astype(bf16)
+    cnd_b = cnd.reshape(chunks, n, per, cch).astype(bf16)
+    sig_b = sig.reshape(chunks, n, per, ch).astype(bf16)
+    xsend[:, :, 0:ch] = sig_b[0]
+    for ck in range(chunks):
+        xsend[:, :, ch + ck * cch:ch + (ck + 1) * cch] = cnd_b[ck]
+        if ck > 0:
+            bsend[ck - 1, :, :, 0:ch] = sig_b[ck]
     h3[...] = sig
 
     pl.semaphore_wait(barrier, n - 1)
@@ -116,8 +121,7 @@
 
     for d in order:
         to = lax.rem(me + d, n)
-        push(csend.at[:, to], crecv.at[:, me], x_send.at[chunks], x_recv.at[chunks], d, to)
-        push(ssend.at[0, to], srecv.at[0, me], x_send.at[0], x_recv.at[0], d, to)
+        push(xsend.at[to], xrecv.at[me], x_send, x_recv, d, to)
     fetch(*range(1, NEAR + 2))
 
     for cp in halo_copies():
@@ -181,13 +185,17 @@
             a, dk = near_layer(k, jnp.where(edge, h0[part] + acc, 0.0), call[part], k < NEAR - 1)
             gates[k, out] = a[:rows]
             acc = acc[:dk.shape[0]] + dk
-        dsend[ck] = acc.reshape(n, per, ch).astype(TRAVEL)
+        if ck == 0:
+            dsend[...] = acc.reshape(n, per, ch).astype(TRAVEL)
+        else:
+            bsend[ck - 1, :, :, ch:2 * ch] = acc.reshape(n, per, ch).astype(TRAVEL)
         near[out] = acc
         for d in order:
             to = lax.rem(me + d, n)
-            if ck > 0:
-                push(ssend.at[ck, to], srecv.at[ck, me], x_send.at[ck], x_recv.at[ck], d, to)
-            push(dsend.at[ck, to], drecv.at[ck, me], d_send, d_recv.at[ck], d, to)
+            if ck == 0:
+                push(dsend.at[to], drecv.at[me], d_send.at[0], d_recv.at[0], d, to)
+            else:
+                push(bsend.at[ck - 1, to], brecv.at[ck - 1, me], d_send.at[ck], d_recv.at[ck], d, to)
         if ck == 0:
             fetch(NEAR + 2, NEAR + 3)
     fetch(*range(NEAR + 4, layers))
@@ -197,13 +205,17 @@
         skp = skp + jnp.dot(gates[k], w2[k, :, ch:wide], preferred_element_type=f32)
     s3[...] = skp
     h3[...] += near[...]
-    drain(crecv, x_recv.at[chunks])
     row = _iota((rows, ch), 0)
     for ck in range(chunks):
-        drain(srecv.at[ck], x_recv.at[ck])
-        drain(drecv.at[ck], d_recv.at[ck])
-        base = (srecv[ck].astype(f32) + drecv[ck].astype(f32)).reshape(rows, ch)
-        cq = crecv[ck].astype(f32).reshape(rows, cch).astype(bf16)
+        if ck == 0:
+            drain(xrecv, x_recv)
+            drain(drecv, d_recv.at[0])
+            base = xrecv[:, :, 0:ch].astype(f32) + drecv[...].astype(f32)
+        else:
+            drain(brecv.at[ck - 1], d_recv.at[ck])
+            base = brecv[ck - 1, :, :, 0:ch].astype(f32) + brecv[ck - 1, :, :, ch:2 * ch].astype(f32)
+        base = base.reshape(rows, ch)
+        cq = xrecv[:, :, ch + ck * cch:ch + (ck + 1) * cch].astype(f32).reshape(rows, cch).astype(bf16)
         h = base
         for k in range(NEAR, layers):
             sft = 2 ** (k - NEAR)
@@ -230,10 +242,11 @@
 
     for cp in halo_copies():
         cp.wait_send()
-    for ck in range(chunks):
-        drain(ssend.at[ck, pl.ds(0, n - 1)], x_send.at[ck])
-    for buf, sem in ((csend.at[:, pl.ds(0, n - 1)], x_send.at[chunks]), (dsend.at[:, pl.ds(0, n - 1)], d_send), (osend.at[:, pl.ds(0, n - 1)], o_send)):
+    for buf, sem in ((xsend.at[pl.ds(0, n - 1)], x_send), (dsend.at[pl.ds(0, n - 1)], d_send.at[0]),
+                     (osend.at[:, pl.ds(0, n - 1)], o_send)):
         drain(buf, sem)
+    for ck in range(1, chunks):
+        drain(bsend.at[ck - 1, pl.ds(0, n - 1)], d_send.at[ck])
     for ck in range(chunks):
         drain(recv.at[ck], o_recv.at[ck])
 
@@ -289,13 +302,13 @@
                 pltpu.VMEM((layers, 2 * ch), f32),
                 pltpu.VMEM((NEAR, own, ch), bf16),
                 pltpu.VMEM((own, ch), f32),
-                pltpu.VMEM((chunks, n, per, ch), bf16), pltpu.VMEM((chunks, n, per, cch), bf16),
-                pltpu.VMEM((chunks, n, per, ch), TRAVEL),
-                pltpu.VMEM((chunks, n, per, ch), bf16), pltpu.VMEM((chunks, n, per, cch), bf16),
-                pltpu.VMEM((chunks, n, per, ch), TRAVEL),
+                pltpu.VMEM((n, per, ch + chunks * cch), bf16), pltpu.VMEM((n, per, ch), TRAVEL),
+                pltpu.VMEM((chunks - 1, n, per, 2 * ch), bf16),
+                pltpu.VMEM((n, per, ch + chunks * cch), bf16), pltpu.VMEM((n, per, ch), TRAVEL),
+                pltpu.VMEM((chunks - 1, n, per, 2 * ch), bf16),
                 pltpu.VMEM((rows, wide), f32), pltpu.VMEM((chunks, n, per, wide), TRAVEL),
-                dma((layers, 5)), dma((3,)), dma((2,)), dma((2,)), dma((chunks + 1,)), dma((chunks + 1,)),
-                dma, dma((chunks,)), dma, dma((chunks,)),
+                dma((layers, 5)), dma((3,)), dma((2,)), dma((2,)), dma, dma,
+                dma((chunks,)), dma((chunks,)), dma, dma((chunks,)),
             ],
             compiler_params=pltpu.CompilerParams(collective_id=0, has_side_effects=True,
                                                  vmem_limit_bytes=56 * 1024 * 1024),

time: 42 us -> 41.6 us (level)
  no operation moved by 1% of the time
where the time goes in v13:
time: 41.6 us; the launch traced here: 41.5 us
  Pallas kernels  40.7 us (98%)
  between operations  0.8 us (2%)
    pallas_call x1, Pallas kernels, local_stack(): pl.pallas_call(functools.partial(_stack, n), name='stack', out_shape=(plt...  39.8 us
    pallas_call x1, Pallas kernels, local_stack(): pl.pallas_call(_finish, name='finish', out_shape=(sds((own, ch), f32), sd...  0.95 us

profile of v13, /device:TPU:21, one launch (start us, length us, event | category | flops | bytes accessed | tf_op | source)
XLA Modules:
  0.0 41.5 jit_solution(502474806028207839)
XLA Ops:
  0.6 39.8 %stack.1 = (bf16[2,16,8,768]{3,2,1,0:T(8,128)(2,1)S(1)}, f32[256,512]{1,0:T(8,128)S(1)}, f32[256,256]{1,0:T(8,128)S(1)}) custom-call(bf16[4,64,512]{2,1,0:T(8,128)(2,1)} %sig_hbm.1, bf16[4,64,128]{2,1,0:T(8,128)(2,1)} %cond_hbm.1, bf16[10,512,1024]{2,1,0:T(8,128)(2,1)} %wn_hbm.1, bf16[10,512,1024]{2,1,0:T(8,128)(2,1)} %wp_hbm.1, ...), custom_call_target="tpu_custom_call" | custom-call | tf_op jit(solution)/shard_map/stack/pallas_call | solution.py:292
  40.4 1.0 %finish.1 = (f32[256,512]{1,0:T(8,128)}, f32[256,256]{1,0:T(8,128)}) custom-call(bf16[2,16,8,768]{3,2,1,0:T(8,128)(2,1)S(1)} %get-tuple-element.7.recv, f32[256,512]{1,0:T(8,128)S(1)} %get-tuple-element.8.h3, f32[256,256]{1,0:T(8,128)S(1)} %get-tuple-element.9.s3), custom_call_target="tpu_custom_call" | custom-call | tf_op jit(solution)/shard_map/finish/pallas_call | solution.py:316

commit v14 on v13

--- a/solution.py
+++ b/solution.py
@@ -196,9 +196,7 @@
                 push(dsend.at[to], drecv.at[me], d_send.at[0], d_recv.at[0], d, to)
             else:
                 push(bsend.at[ck - 1, to], brecv.at[ck - 1, me], d_send.at[ck], d_recv.at[ck], d, to)
-        if ck == 0:
-            fetch(NEAR + 2, NEAR + 3)
-    fetch(*range(NEAR + 4, layers))
+    fetch(*range(NEAR + 2, layers))
 
     skp = jnp.dot(gates[0], w2[0, :, ch:wide], preferred_element_type=f32)
     for k in range(1, NEAR):

time: 41.6 us -> 41.8 us (level)
  no operation moved by 1% of the time
where the time goes in v14:
time: 41.8 us; the launch traced here: 41.7 us
  Pallas kernels  40.9 us (98%)
  between operations  0.8 us (2%)
    pallas_call x1, Pallas kernels, local_stack(): pl.pallas_call(functools.partial(_stack, n), name='stack', out_shape=(plt...  40 us
    pallas_call x1, Pallas kernels, local_stack(): pl.pallas_call(_finish, name='finish', out_shape=(sds((own, ch), f32), sd...  0.95 us

profile of v14, /device:TPU:21, one launch (start us, length us, event | category | flops | bytes accessed | tf_op | source)
XLA Modules:
  0.0 41.7 jit_solution(7873816122236684336)
XLA Ops:
  0.6 40.0 %stack.1 = (bf16[2,16,8,768]{3,2,1,0:T(8,128)(2,1)S(1)}, f32[256,512]{1,0:T(8,128)S(1)}, f32[256,256]{1,0:T(8,128)S(1)}) custom-call(bf16[4,64,512]{2,1,0:T(8,128)(2,1)} %sig_hbm.1, bf16[4,64,128]{2,1,0:T(8,128)(2,1)} %cond_hbm.1, bf16[10,512,1024]{2,1,0:T(8,128)(2,1)} %wn_hbm.1, bf16[10,512,1024]{2,1,0:T(8,128)(2,1)} %wp_hbm.1, ...), custom_call_target="tpu_custom_call" | custom-call | tf_op jit(solution)/shard_map/stack/pallas_call | solution.py:290
  40.6 1.0 %finish.1 = (f32[256,512]{1,0:T(8,128)}, f32[256,256]{1,0:T(8,128)}) custom-call(bf16[2,16,8,768]{3,2,1,0:T(8,128)(2,1)S(1)} %get-tuple-element.7.recv, f32[256,512]{1,0:T(8,128)S(1)} %get-tuple-element.8.h3, f32[256,256]{1,0:T(8,128)S(1)} %get-tuple-element.9.s3), custom_call_target="tpu_custom_call" | custom-call | tf_op jit(solution)/shard_map/finish/pallas_call | solution.py:314
